TPU v7x, 32 devices: a whole 2x2x4 slice. The times are simulated.
32 devices in a mesh: groups: 2 (over x), bay: 16 (over z, y, core).
Axes of the slice: x: 2, y: 2, z: 4, core: 2. Of those that a mesh axis runs over, the one named last changes fastest.
Arguments:
- traces: bfloat16 [16, 512, 2048], P('bay', 'groups'), parts along dimension 1, may hold values from -6 to 6
- operator: bfloat16 [16, 2048, 2048], P('bay'), may hold values from -0.09375 to 0.09375
- loads: bfloat16 [16, 16, 2048], P('bay'), may hold values from -6 to 6
- seeds: int32 [512], P('groups'), parts along dimension 0, may hold values from 0 to 99999
- patches: int32 [16, 512], P('bay', 'groups'), parts along dimension 1, may hold values from 0 to 15
- trace_map: int32 [16, 1024], P('bay'), may hold values from 0 to 1023, each once within a row
Outputs:
- final_traces: bfloat16 [16, 512, 2048], P('bay', 'groups'), parts along dimension 1
There are 2 independent parts, one for each index of `groups`. A program takes and returns all parts, laid end to end along the dimension named above; an argument that names none is the same for every part. Nothing has to cross between parts.
Inputs may be any that keep to these rules, and one draw needn't show every extreme that they name: `trace_map`: each row is a permutation of 0 to 1023.
All inputs are finite; a program needn't handle non-finite values.
Results may differ from a plain program's by a relative error of at most 0.0065.
Values may be sent and summed in bfloat16 or wider, within the bound.
No kernel may reach another device: no remote copies, remote signals or barrier semaphores. Data moves between devices by JAX's collectives and lax.ppermute only.
A program may use at most 64 MiB of HBM per device.

v0:
```python
import functools

import jax
import jax.numpy as jnp
from jax import lax
from jax.experimental import pallas as pl
from jax.experimental.pallas import tpu as pltpu
from jax.sharding import PartitionSpec as P


TICKS = 6
STRIPS = 4
CHUNKS = 2
COLS = 512
EARLY = 6
LIMIT = 16 << 20


VMEM = pl.BlockSpec(memory_space=pltpu.VMEM)
HBM = pl.BlockSpec(memory_space=pltpu.HBM)
ANY = pl.BlockSpec(memory_space=pl.ANY)


def exchange(pieces, count, wrap=True):
    onward, near, far = pieces
    stop = count if wrap else count - STRIPS
    got_onward = lax.ppermute(
        onward, "bay", [(i, (i + STRIPS) % count) for i in range(stop)]
    )
    got_near = lax.ppermute(near, "bay", [(i, i ^ 1) for i in range(count)])
    got_far = lax.ppermute(far, "bay", [(i, i ^ 2) for i in range(count)])
    return got_onward, got_near, got_far


def fetch(source, outs, spans, sems):
    copies = []
    for index, (out, (rows, columns)) in enumerate(zip(outs, spans)):
        copies.append(pltpu.make_async_copy(source.at[0, rows, columns], out, sems.at[index]))
        copies[-1].start()
    return copies


def cut_body(spans, source, *rest):
    *outs, sems = rest
    for copy in fetch(source, outs, spans, sems):
        copy.wait()


def load_body(spans, trace_map, source, operator, table, *rest):
    *outs, select, weights, loads, order, sems = rest
    fetch_order = pltpu.make_async_copy(trace_map, order, sems.at[len(spans) + 2])
    fetch_order.start()
    copies = fetch(source, outs, spans, sems)
    for index, (whole, out) in enumerate(((operator, weights), (table, loads))):
        copies.append(pltpu.make_async_copy(whole.at[0], out, sems.at[len(spans) + index]))
        copies[-1].start()
    size = order.shape[1]
    block = min(256, size)
    fetch_order.wait()
    wanted = jnp.where(lax.axis_index("bay") >= STRIPS, order[...], -1)
    for top in range(0, size, block):
        rows = top + lax.broadcasted_iota(jnp.int32, (block, size), 0)
        select[top : top + block, :] = (wanted == rows).astype(jnp.bfloat16)
    for copy in copies:
        copy.wait()


def shape_of(span):
    return jax.ShapeDtypeStruct(tuple(part.stop - part.start for part in span), jnp.bfloat16)


def in_hbm(*arrays):
    return [pltpu.with_memory_space_constraint(array, pltpu.HBM) for array in arrays]


def cut(traces, spans):
    return pl.pallas_call(
        functools.partial(cut_body, spans),
        out_shape=tuple(shape_of(span) for span in spans),
        in_specs=[HBM],
        out_specs=(VMEM,) * len(spans),
        scratch_shapes=[pltpu.SemaphoreType.DMA((len(spans),))],
        name="cut",
        compiler_params=pltpu.CompilerParams(vmem_limit_bytes=LIMIT),
    )(*in_hbm(traces))


def load(order, traces, spans, operator, loads):
    shapes = [shape_of(span) for span in spans]
    shapes.append(jax.ShapeDtypeStruct((order.shape[1],) * 2, jnp.bfloat16))
    shapes.extend(jax.ShapeDtypeStruct(whole.shape[1:], jnp.bfloat16) for whole in (operator, loads))
    return pl.pallas_call(
        functools.partial(load_body, spans),
        out_shape=tuple(shapes),
        in_specs=[HBM] * 4,
        out_specs=(VMEM,) * len(shapes),
        scratch_shapes=[
            pltpu.VMEM(order.shape, order.dtype),
            pltpu.SemaphoreType.DMA((len(spans) + 3,)),
        ],
        name="load",
        compiler_params=pltpu.CompilerParams(vmem_limit_bytes=LIMIT),
    )(*in_hbm(order, traces, operator, loads))


def prepared(tick, chunk, onward, select, seeds, patches, table):
    size = onward.shape[0]
    own = slice(chunk * size, (chunk + 1) * size)
    mapped = jnp.dot(onward[...], select[...], preferred_element_type=jnp.float32).astype(
        jnp.bfloat16
    )
    amplitude = ((seeds[:, own] * 7 + 13 * tick) % 97 - 48).astype(jnp.float32) / 32.0
    rows = lax.broadcasted_iota(jnp.int32, (table.shape[0], size), 0)
    loaded = jnp.where(rows == patches[:, own], amplitude, 0.0).astype(jnp.bfloat16)
    return mapped, loaded


def block(mapped, loaded, near, far, weights, table, low, high):
    first = mapped.shape[1]
    second = first + near.shape[1]
    total = jnp.dot(near[...], weights[first:second, low:high], preferred_element_type=jnp.float32)
    total += jnp.dot(far[...], weights[second:, low:high], preferred_element_type=jnp.float32)
    total += lax.dot_general(
        loaded, table[:, low:high], (((0,), (0,)), ((), ())), preferred_element_type=jnp.float32
    )
    total += jnp.dot(mapped, weights[:first, low:high], preferred_element_type=jnp.float32)
    return total.astype(jnp.bfloat16)


def step_body(tick, chunk, onward, near, far, select, seeds, patches, table, weights, *outs):
    mapped, loaded = prepared(tick, chunk, onward, select, seeds, patches, table)
    start = 0
    for out in outs:
        for low in range(0, out.shape[1], COLS):
            out[:, low : low + COLS] = block(
                mapped, loaded, near, far, weights, table, start + low, start + low + COLS
            )
        start += out.shape[1]


def cost(rows, weights):
    return pl.CostEstimate(
        flops=2 * rows * weights.shape[0] * weights.shape[1],
        transcendentals=0,
        bytes_accessed=weights.size * 2,
    )


def step(tick, chunk, got, common, weights):
    return pl.pallas_call(
        functools.partial(step_body, tick, chunk),
        out_shape=tuple(jax.ShapeDtypeStruct(piece.shape, jnp.bfloat16) for piece in got),
        in_specs=[VMEM] * 8,
        out_specs=(VMEM,) * 3,
        compiler_params=pltpu.CompilerParams(vmem_limit_bytes=LIMIT),
        cost_estimate=cost(got[0].shape[0], weights),
    )(*got, *common, weights)


def last_body(tick, chunk, onward, near, far, select, seeds, patches, table, weights, *rest):
    out, buffer, sems = rest[-3:]
    rows, width = buffer.shape
    mapped, loaded = prepared(tick, chunk, onward, select, seeds, patches, table)
    copies = []
    for index, low in enumerate(range(0, width, COLS)):
        buffer[:, low : low + COLS] = block(
            mapped, loaded, near, far, weights, table, low, low + COLS
        )
        copies.append(
            pltpu.make_async_copy(
                buffer.at[:, low : low + COLS],
                out.at[0, chunk * rows : (chunk + 1) * rows, low : low + COLS],
                sems.at[index],
            )
        )
        copies[-1].start()
    for copy in copies:
        copy.wait()


def last_step(tick, chunk, got, common, weights, previous):
    rows, width = got[0].shape[0], weights.shape[1]
    extra = [] if previous is None else [previous]
    return pl.pallas_call(
        functools.partial(last_body, tick, chunk),
        out_shape=jax.ShapeDtypeStruct((1, rows * CHUNKS, width), jnp.bfloat16),
        in_specs=[VMEM] * 8 + [ANY] * len(extra),
        out_specs=ANY,
        scratch_shapes=[
            pltpu.VMEM((rows, width), jnp.bfloat16),
            pltpu.SemaphoreType.DMA((pl.cdiv(width, COLS),)),
        ],
        input_output_aliases={8: 0} if extra else {},
        name="last",
        compiler_params=pltpu.CompilerParams(vmem_limit_bytes=LIMIT),
        cost_estimate=cost(rows, weights),
    )(*got, *common, weights, *extra)


def on_device(traces, operator, loads, seeds, patches, trace_map):
    count = lax.axis_size("bay")
    _, rows, width = traces.shape
    onward = trace_map.shape[1]
    near = onward + (width - onward) // 2
    size = rows // CHUNKS
    columns = (slice(0, onward), slice(onward, near), slice(near, width))
    spans = [
        [(slice(c * size, (c + 1) * size), piece) for piece in columns] for c in range(CHUNKS)
    ]
    flat = [span for part in spans for span in part]

    pieces = cut(traces, flat[:EARLY])
    *others, select, weights, table = load(trace_map, traces, flat[EARLY:], operator, loads)
    pieces = [*pieces, *others]
    got = []
    for c in range(CHUNKS):
        got.append(exchange(pieces[3 * c : 3 * c + 3], count))

    common = (select, seeds[None], patches, table)
    out = None
    for tick in range(TICKS):
        for c in range(CHUNKS):
            if tick == TICKS - 1:
                out = last_step(tick, c, got[c], common, weights, out)
            else:
                pieces = step(tick, c, got[c], common, weights)
                got[c] = exchange(pieces, count, tick + 2 < TICKS)
    return out


def solution(mesh):
    placed = (
        P("bay", "groups", None),
        P("bay", None, None),
        P("bay", None, None),
        P("groups"),
        P("bay", "groups"),
        P("bay", None),
    )
    return jax.shard_map(
        on_device, mesh=mesh, in_specs=placed, out_specs=P("bay", "groups", None), check_vma=False
    )
```

profile of v0, /device:TPU:0, one launch (start us, length us, event | category | flops | bytes accessed | tf_op | source)
XLA Modules:
  0.0 85.0 jit_solution(3475710325549919671)
XLA Ops:
  1.3 3.1 %collective-permute-start.18 = (bf16[128,1024]{1,0:T(8,128)(2,1)S(1)}, bf16[128,1024]{1,0:T(8,128)(2,1)S(1)}, u32[]{:S(2)}, u32[]{:S(2)}) collective-permute-start(bf16[128,1024]{1,0:T(8,128)(2,1)S(1)} %get-tuple-element.65), channel_id=1, source_target_pairs={{0,4},{1,5},{2,6},{3,7},{4,8},{5,9},{6,10},{7,11},{8,12},{9,13},{1... | collective-permute-start | bytes 786440 | tf_op jit(solution)/shard_map/ppermute | solution.py:27
  8.0 3.4 %load.1 = (bf16[1024,1024]{1,0:T(8,128)(2,1)S(1)}, bf16[2048,2048]{1,0:T(8,128)(2,1)S(1)}, bf16[16,2048]{1,0:T(8,128)(2,1)S(1)}) custom-call(s32[1,1024]{1,0:T(1,128)} %trace_map.1, bf16[1,256,2048]{2,1,0:T(8,128)(2,1)} %source.3, bf16[1,2048,2048]{2,1,0:T(8,128)(2,1)} %operator.1, bf16[1,16,2048]{2,1,0:T(8,128)(2,1)} %table.1), custom_call_target="tpu_custom_call" | custom-call | tf_op jit(solution)/shard_map/load/pallas_call | solution.py:92
  13.6 1.7 %shard_map.69 = (bf16[128,1024]{1,0:T(8,128)(2,1)S(1)}, bf16[128,512]{1,0:T(8,128)(2,1)S(1)}, bf16[128,512]{1,0:T(8,128)(2,1)S(1)}) custom-call(bf16[128,1024]{1,0:T(8,128)(2,1)S(1)} %collective-permute-done.18.onward, bf16[128,512]{1,0:T(8,128)(2,1)S(1)} %collective-permute-done.19.near, bf16[128,512]{1,0:T(8,128)(2,1)S(1)} %collective-permute-done.20.far, ...), custom_call_target="tpu_custom_call" | custom-call | flops 1073741824 | bytes 8388608 | tf_op jit(solution)/shard_map/pallas_call | solution.py:150
  15.7 2.9 %collective-permute-done.onward = bf16[128,1024]{1,0:T(8,128)(2,1)S(1)} collective-permute-done((bf16[128,1024]{1,0:T(8,128)(2,1)S(1)}, bf16[128,1024]{1,0:T(8,128)(2,1)S(1)}, u32[]{:S(2)}, u32[]{:S(2)}) %collective-permute-start) | collective-permute-done | bytes 262176 | tf_op jit(solution)/shard_map/ppermute | solution.py:27
  20.3 1.8 %collective-permute-start.23 = (bf16[128,512]{1,0:T(8,128)(2,1)S(1)}, bf16[128,512]{1,0:T(8,128)(2,1)S(1)}, u32[]{:S(2)}, u32[]{:S(2)}) collective-permute-start(bf16[128,512]{1,0:T(8,128)(2,1)S(1)} %get-tuple-element.70), channel_id=1, source_target_pairs={{0,2},{1,3},{2,0},{3,1},{4,6},{5,7},{6,4},{7,5},{8,10},{9,11},{10,... | collective-permute-start | bytes 393224 | tf_op jit(solution)/shard_map/ppermute | solution.py:31
  22.4 3.4 %collective-permute-done.23.far = bf16[128,512]{1,0:T(8,128)(2,1)S(1)} collective-permute-done((bf16[128,512]{1,0:T(8,128)(2,1)S(1)}, bf16[128,512]{1,0:T(8,128)(2,1)S(1)}, u32[]{:S(2)}, u32[]{:S(2)}) %collective-permute-start.23) | collective-permute-done | bytes 131104 | tf_op jit(solution)/shard_map/ppermute | solution.py:31
  27.6 2.1 %collective-permute-start.24 = (bf16[128,1024]{1,0:T(8,128)(2,1)S(1)}, bf16[128,1024]{1,0:T(8,128)(2,1)S(1)}, u32[]{:S(2)}, u32[]{:S(2)}) collective-permute-start(bf16[128,1024]{1,0:T(8,128)(2,1)S(1)} %get-tuple-element.71), channel_id=1, source_target_pairs={{0,4},{1,5},{2,6},{3,7},{4,8},{5,9},{6,10},{7,11},{8,12},{9,13},{1... | collective-permute-start | bytes 786440 | tf_op jit(solution)/shard_map/ppermute | solution.py:27
  29.7 1.7 %shard_map.65 = (bf16[128,1024]{1,0:T(8,128)(2,1)S(1)}, bf16[128,512]{1,0:T(8,128)(2,1)S(1)}, bf16[128,512]{1,0:T(8,128)(2,1)S(1)}) custom-call(bf16[128,1024]{1,0:T(8,128)(2,1)S(1)} %collective-permute-done.3.onward, bf16[128,512]{1,0:T(8,128)(2,1)S(1)} %collective-permute-done.4.near, bf16[128,512]{1,0:T(8,128)(2,1)S(1)} %collective-permute-done.5.far, ...), custom_call_target="tpu_custom_call" | custom-call | flops 1073741824 | bytes 8388608 | tf_op jit(solution)/shard_map/pallas_call | solution.py:150
  33.0 2.5 %collective-permute-start.26 = (bf16[128,512]{1,0:T(8,128)(2,1)S(1)}, bf16[128,512]{1,0:T(8,128)(2,1)S(1)}, u32[]{:S(2)}, u32[]{:S(2)}) collective-permute-start(bf16[128,512]{1,0:T(8,128)(2,1)S(1)} %get-tuple-element.73), channel_id=1, source_target_pairs={{0,2},{1,3},{2,0},{3,1},{4,6},{5,7},{6,4},{7,5},{8,10},{9,11},{10,... | collective-permute-start | bytes 393224 | tf_op jit(solution)/shard_map/ppermute | solution.py:31
  35.7 4.1 %collective-permute-done.26.far = bf16[128,512]{1,0:T(8,128)(2,1)S(1)} collective-permute-done((bf16[128,512]{1,0:T(8,128)(2,1)S(1)}, bf16[128,512]{1,0:T(8,128)(2,1)S(1)}, u32[]{:S(2)}, u32[]{:S(2)}) %collective-permute-start.26) | collective-permute-done | bytes 131104 | tf_op jit(solution)/shard_map/ppermute | solution.py:31
  42.9 1.7 %shard_map.66 = (bf16[128,1024]{1,0:T(8,128)(2,1)S(1)}, bf16[128,512]{1,0:T(8,128)(2,1)S(1)}, bf16[128,512]{1,0:T(8,128)(2,1)S(1)}) custom-call(bf16[128,1024]{1,0:T(8,128)(2,1)S(1)} %collective-permute-done.6.onward, bf16[128,512]{1,0:T(8,128)(2,1)S(1)} %collective-permute-done.7.near, bf16[128,512]{1,0:T(8,128)(2,1)S(1)} %collective-permute-done.8.far, ...), custom_call_target="tpu_custom_call" | custom-call | flops 1073741824 | bytes 8388608 | tf_op jit(solution)/shard_map/pallas_call | solution.py:150
  45.4 1.8 %collective-permute-start.29 = (bf16[128,512]{1,0:T(8,128)(2,1)S(1)}, bf16[128,512]{1,0:T(8,128)(2,1)S(1)}, u32[]{:S(2)}, u32[]{:S(2)}) collective-permute-start(bf16[128,512]{1,0:T(8,128)(2,1)S(1)} %get-tuple-element.76), channel_id=1, source_target_pairs={{0,2},{1,3},{2,0},{3,1},{4,6},{5,7},{6,4},{7,5},{8,10},{9,11},{10,... | collective-permute-start | bytes 393224 | tf_op jit(solution)/shard_map/ppermute | solution.py:31
  47.5 4.3 %collective-permute-done.29.far = bf16[128,512]{1,0:T(8,128)(2,1)S(1)} collective-permute-done((bf16[128,512]{1,0:T(8,128)(2,1)S(1)}, bf16[128,512]{1,0:T(8,128)(2,1)S(1)}, u32[]{:S(2)}, u32[]{:S(2)}) %collective-permute-start.29) | collective-permute-done | bytes 131104 | tf_op jit(solution)/shard_map/ppermute | solution.py:31
  51.9 1.7 %shard_map.72 = (bf16[128,1024]{1,0:T(8,128)(2,1)S(1)}, bf16[128,512]{1,0:T(8,128)(2,1)S(1)}, bf16[128,512]{1,0:T(8,128)(2,1)S(1)}) custom-call(bf16[128,1024]{1,0:T(8,128)(2,1)S(1)} %collective-permute-done.27.onward, bf16[128,512]{1,0:T(8,128)(2,1)S(1)} %collective-permute-done.28.near, bf16[128,512]{1,0:T(8,128)(2,1)S(1)} %collective-permute-done.29.far, ...), custom_call_target="tpu_custom_call" | custom-call | flops 1073741824 | bytes 8388608 | tf_op jit(solution)/shard_map/pallas_call | solution.py:150
  58.4 2.0 %collective-permute-start.32 = (bf16[128,512]{1,0:T(8,128)(2,1)S(1)}, bf16[128,512]{1,0:T(8,128)(2,1)S(1)}, u32[]{:S(2)}, u32[]{:S(2)}) collective-permute-start(bf16[128,512]{1,0:T(8,128)(2,1)S(1)} %get-tuple-element.79), channel_id=1, source_target_pairs={{0,2},{1,3},{2,0},{3,1},{4,6},{5,7},{6,4},{7,5},{8,10},{9,11},{10,... | collective-permute-start | bytes 393224 | tf_op jit(solution)/shard_map/ppermute | solution.py:31
  60.7 4.1 %collective-permute-done.32.far = bf16[128,512]{1,0:T(8,128)(2,1)S(1)} collective-permute-done((bf16[128,512]{1,0:T(8,128)(2,1)S(1)}, bf16[128,512]{1,0:T(8,128)(2,1)S(1)}, u32[]{:S(2)}, u32[]{:S(2)}) %collective-permute-start.32) | collective-permute-done | bytes 131104 | tf_op jit(solution)/shard_map/ppermute | solution.py:31
  64.8 1.7 %shard_map.73 = (bf16[128,1024]{1,0:T(8,128)(2,1)S(1)}, bf16[128,512]{1,0:T(8,128)(2,1)S(1)}, bf16[128,512]{1,0:T(8,128)(2,1)S(1)}) custom-call(bf16[128,1024]{1,0:T(8,128)(2,1)S(1)} %collective-permute-done.30.onward, bf16[128,512]{1,0:T(8,128)(2,1)S(1)} %collective-permute-done.31.near, bf16[128,512]{1,0:T(8,128)(2,1)S(1)} %collective-permute-done.32.far, ...), custom_call_target="tpu_custom_call" | custom-call | flops 1073741824 | bytes 8388608 | tf_op jit(solution)/shard_map/pallas_call | solution.py:150
  66.6 3.2 %collective-permute-start.33 = (bf16[128,1024]{1,0:T(8,128)(2,1)S(1)}, bf16[128,1024]{1,0:T(8,128)(2,1)S(1)}, u32[]{:S(2)}, u32[]{:S(2)}) collective-permute-start(bf16[128,1024]{1,0:T(8,128)(2,1)S(1)} %get-tuple-element.80), channel_id=1, source_target_pairs={{0,4},{1,5},{2,6},{3,7},{4,8},{5,9},{6,10},{7,11},{8,12},{9,13},{1... | collective-permute-start | bytes 786440 | tf_op jit(solution)/shard_map/ppermute | solution.py:27
  69.8 1.7 %shard_map.68 = (bf16[128,1024]{1,0:T(8,128)(2,1)S(1)}, bf16[128,512]{1,0:T(8,128)(2,1)S(1)}, bf16[128,512]{1,0:T(8,128)(2,1)S(1)}) custom-call(bf16[128,1024]{1,0:T(8,128)(2,1)S(1)} %collective-permute-done.12.onward, bf16[128,512]{1,0:T(8,128)(2,1)S(1)} %collective-permute-done.13.near, bf16[128,512]{1,0:T(8,128)(2,1)S(1)} %collective-permute-done.14.far, ...), custom_call_target="tpu_custom_call" | custom-call | flops 1073741824 | bytes 8388608 | tf_op jit(solution)/shard_map/pallas_call | solution.py:150
  71.5 2.6 %collective-permute-start.15 = (bf16[128,1024]{1,0:T(8,128)(2,1)S(1)}, bf16[128,1024]{1,0:T(8,128)(2,1)S(1)}, u32[]{:S(2)}, u32[]{:S(2)}) collective-permute-start(bf16[128,1024]{1,0:T(8,128)(2,1)S(1)} %get-tuple-element.62), channel_id=1, source_target_pairs={{0,4},{1,5},{2,6},{3,7},{4,8},{5,9},{6,10},{7,11},{8,12},{9,13},{1... | collective-permute-start | bytes 786440 | tf_op jit(solution)/shard_map/ppermute | solution.py:27
  74.1 1.7 %collective-permute-start.35 = (bf16[128,512]{1,0:T(8,128)(2,1)S(1)}, bf16[128,512]{1,0:T(8,128)(2,1)S(1)}, u32[]{:S(2)}, u32[]{:S(2)}) collective-permute-start(bf16[128,512]{1,0:T(8,128)(2,1)S(1)} %get-tuple-element.82), channel_id=1, source_target_pairs={{0,2},{1,3},{2,0},{3,1},{4,6},{5,7},{6,4},{7,5},{8,10},{9,11},{10,... | collective-permute-start | bytes 393224 | tf_op jit(solution)/shard_map/ppermute | solution.py:31
  76.2 3.9 %collective-permute-done.35.far = bf16[128,512]{1,0:T(8,128)(2,1)S(1)} collective-permute-done((bf16[128,512]{1,0:T(8,128)(2,1)S(1)}, bf16[128,512]{1,0:T(8,128)(2,1)S(1)}, u32[]{:S(2)}, u32[]{:S(2)}) %collective-permute-start.35) | collective-permute-done | bytes 131104 | tf_op jit(solution)/shard_map/ppermute | solution.py:31
  80.0 2.4 %last.2.rest_0_ = bf16[1,256,2048]{2,1,0:T(8,128)(2,1)} custom-call(bf16[128,1024]{1,0:T(8,128)(2,1)S(1)} %collective-permute-done.33.onward, bf16[128,512]{1,0:T(8,128)(2,1)S(1)} %collective-permute-done.34.near, bf16[128,512]{1,0:T(8,128)(2,1)S(1)} %collective-permute-done.35.far, bf16[1024,1024]{1,0:T(8,128)(2,1)S(1)} %get-tuple-element.47.select, ...), custom_call_target="tpu_custom_call" | custom-call | flops 1073741824 | bytes 8388608 | tf_op jit(solution)/shard_map/last/pallas_call | solution.py:184
  82.5 2.4 %last.3 = bf16[1,256,2048]{2,1,0:T(8,128)(2,1)} custom-call(bf16[128,1024]{1,0:T(8,128)(2,1)S(1)} %collective-permute-done.15.onward, bf16[128,512]{1,0:T(8,128)(2,1)S(1)} %collective-permute-done.16.near, bf16[128,512]{1,0:T(8,128)(2,1)S(1)} %collective-permute-done.17.far, ...), custom_call_target="tpu_custom_call", output_to_operand_aliasing={{}: (8, {})} | custom-call | flops 1073741824 | bytes 8388608 | tf_op jit(solution)/shard_map/last/pallas_call | solution.py:184
  (66 shorter events, 22.9 us)
Async XLA Ops:
  1.3 12.3 %collective-permute-start.18 = (bf16[128,1024]{1,0:T(8,128)(2,1)S(1)}, bf16[128,1024]{1,0:T(8,128)(2,1)S(1)}, u32[]{:S(2)}, u32[]{:S(2)}) collective-permute-start(bf16[128,1024]{1,0:T(8,128)(2,1)S(1)} %get-tuple-element.65), channel_id=1, source_target_pairs={{0,4},{1,5},{2,6},{3,7},{4,8},{5,9},{6,10},{7,11},{8,12},{9,13},{1... | collective-permute-start | bytes 786440 | tf_op jit(solution)/shard_map/ppermute | solution.py:27
  4.4 14.2 %collective-permute-start = (bf16[128,1024]{1,0:T(8,128)(2,1)S(1)}, bf16[128,1024]{1,0:T(8,128)(2,1)S(1)}, u32[]{:S(2)}, u32[]{:S(2)}) collective-permute-start(bf16[128,1024]{1,0:T(8,128)(2,1)S(1)} %get-tuple-element.44), channel_id=1, source_target_pairs={{0,4},{1,5},{2,6},{3,7},{4,8},{5,9},{6,10},{7,11},{8,12},{9,13},{1... | collective-permute-start | bytes 786440 | tf_op jit(solution)/shard_map/ppermute | solution.py:27
  7.5 8.2 %collective-permute-start.1 = (bf16[128,512]{1,0:T(8,128)(2,1)S(1)}, bf16[128,512]{1,0:T(8,128)(2,1)S(1)}, u32[]{:S(2)}, u32[]{:S(2)}) collective-permute-start(bf16[128,512]{1,0:T(8,128)(2,1)S(1)} %get-tuple-element.45), channel_id=1, source_target_pairs={{0,1},{1,0},{2,3},{3,2},{4,5},{5,4},{6,7},{7,6},{8,9},{9,8},{10,11... | collective-permute-start | bytes 393224 | tf_op jit(solution)/shard_map/ppermute | solution.py:30
  7.5 8.2 %collective-permute-start.2 = (bf16[128,512]{1,0:T(8,128)(2,1)S(1)}, bf16[128,512]{1,0:T(8,128)(2,1)S(1)}, u32[]{:S(2)}, u32[]{:S(2)}) collective-permute-start(bf16[128,512]{1,0:T(8,128)(2,1)S(1)} %get-tuple-element.46), channel_id=1, source_target_pairs={{0,2},{1,3},{2,0},{3,1},{4,6},{5,7},{6,4},{7,5},{8,10},{9,11},{10,... | collective-permute-start | bytes 393224 | tf_op jit(solution)/shard_map/ppermute | solution.py:31
  15.3 10.6 %collective-permute-start.21 = (bf16[128,1024]{1,0:T(8,128)(2,1)S(1)}, bf16[128,1024]{1,0:T(8,128)(2,1)S(1)}, u32[]{:S(2)}, u32[]{:S(2)}) collective-permute-start(bf16[128,1024]{1,0:T(8,128)(2,1)S(1)} %get-tuple-element.68), channel_id=1, source_target_pairs={{0,4},{1,5},{2,6},{3,7},{4,8},{5,9},{6,10},{7,11},{8,12},{9,13},{1... | collective-permute-start | bytes 786440 | tf_op jit(solution)/shard_map/ppermute | solution.py:27
  20.3 9.4 %collective-permute-start.3 = (bf16[128,1024]{1,0:T(8,128)(2,1)S(1)}, bf16[128,1024]{1,0:T(8,128)(2,1)S(1)}, u32[]{:S(2)}, u32[]{:S(2)}) collective-permute-start(bf16[128,1024]{1,0:T(8,128)(2,1)S(1)} %get-tuple-element.50), channel_id=1, source_target_pairs={{0,4},{1,5},{2,6},{3,7},{4,8},{5,9},{6,10},{7,11},{8,12},{9,13},{1... | collective-permute-start | bytes 786440 | tf_op jit(solution)/shard_map/ppermute | solution.py:27
  22.2 7.5 %collective-permute-start.4 = (bf16[128,512]{1,0:T(8,128)(2,1)S(1)}, bf16[128,512]{1,0:T(8,128)(2,1)S(1)}, u32[]{:S(2)}, u32[]{:S(2)}) collective-permute-start(bf16[128,512]{1,0:T(8,128)(2,1)S(1)} %get-tuple-element.51), channel_id=1, source_target_pairs={{0,1},{1,0},{2,3},{3,2},{4,5},{5,4},{6,7},{7,6},{8,9},{9,8},{10,11... | collective-permute-start | bytes 393224 | tf_op jit(solution)/shard_map/ppermute | solution.py:30
  22.2 7.5 %collective-permute-start.5 = (bf16[128,512]{1,0:T(8,128)(2,1)S(1)}, bf16[128,512]{1,0:T(8,128)(2,1)S(1)}, u32[]{:S(2)}, u32[]{:S(2)}) collective-permute-start(bf16[128,512]{1,0:T(8,128)(2,1)S(1)} %get-tuple-element.52), channel_id=1, source_target_pairs={{0,2},{1,3},{2,0},{3,1},{4,6},{5,7},{6,4},{7,5},{8,10},{9,11},{10,... | collective-permute-start | bytes 393224 | tf_op jit(solution)/shard_map/ppermute | solution.py:31
  27.6 12.3 %collective-permute-start.24 = (bf16[128,1024]{1,0:T(8,128)(2,1)S(1)}, bf16[128,1024]{1,0:T(8,128)(2,1)S(1)}, u32[]{:S(2)}, u32[]{:S(2)}) collective-permute-start(bf16[128,1024]{1,0:T(8,128)(2,1)S(1)} %get-tuple-element.71), channel_id=1, source_target_pairs={{0,4},{1,5},{2,6},{3,7},{4,8},{5,9},{6,10},{7,11},{8,12},{9,13},{1... | collective-permute-start | bytes 786440 | tf_op jit(solution)/shard_map/ppermute | solution.py:27
  31.4 11.5 %collective-permute-start.6 = (bf16[128,1024]{1,0:T(8,128)(2,1)S(1)}, bf16[128,1024]{1,0:T(8,128)(2,1)S(1)}, u32[]{:S(2)}, u32[]{:S(2)}) collective-permute-start(bf16[128,1024]{1,0:T(8,128)(2,1)S(1)} %get-tuple-element.53), channel_id=1, source_target_pairs={{0,4},{1,5},{2,6},{3,7},{4,8},{5,9},{6,10},{7,11},{8,12},{9,13},{1... | collective-permute-start | bytes 786440 | tf_op jit(solution)/shard_map/ppermute | solution.py:27
  33.0 6.8 %collective-permute-start.26 = (bf16[128,512]{1,0:T(8,128)(2,1)S(1)}, bf16[128,512]{1,0:T(8,128)(2,1)S(1)}, u32[]{:S(2)}, u32[]{:S(2)}) collective-permute-start(bf16[128,512]{1,0:T(8,128)(2,1)S(1)} %get-tuple-element.73), channel_id=1, source_target_pairs={{0,2},{1,3},{2,0},{3,1},{4,6},{5,7},{6,4},{7,5},{8,10},{9,11},{10,... | collective-permute-start | bytes 393224 | tf_op jit(solution)/shard_map/ppermute | solution.py:31
  35.5 7.4 %collective-permute-start.7 = (bf16[128,512]{1,0:T(8,128)(2,1)S(1)}, bf16[128,512]{1,0:T(8,128)(2,1)S(1)}, u32[]{:S(2)}, u32[]{:S(2)}) collective-permute-start(bf16[128,512]{1,0:T(8,128)(2,1)S(1)} %get-tuple-element.54), channel_id=1, source_target_pairs={{0,1},{1,0},{2,3},{3,2},{4,5},{5,4},{6,7},{7,6},{8,9},{9,8},{10,11... | collective-permute-start | bytes 393224 | tf_op jit(solution)/shard_map/ppermute | solution.py:30
  35.5 7.4 %collective-permute-start.8 = (bf16[128,512]{1,0:T(8,128)(2,1)S(1)}, bf16[128,512]{1,0:T(8,128)(2,1)S(1)}, u32[]{:S(2)}, u32[]{:S(2)}) collective-permute-start(bf16[128,512]{1,0:T(8,128)(2,1)S(1)} %get-tuple-element.55), channel_id=1, source_target_pairs={{0,2},{1,3},{2,0},{3,1},{4,6},{5,7},{6,4},{7,5},{8,10},{9,11},{10,... | collective-permute-start | bytes 393224 | tf_op jit(solution)/shard_map/ppermute | solution.py:31
  41.5 10.3 %collective-permute-start.27 = (bf16[128,1024]{1,0:T(8,128)(2,1)S(1)}, bf16[128,1024]{1,0:T(8,128)(2,1)S(1)}, u32[]{:S(2)}, u32[]{:S(2)}) collective-permute-start(bf16[128,1024]{1,0:T(8,128)(2,1)S(1)} %get-tuple-element.74), channel_id=1, source_target_pairs={{0,4},{1,5},{2,6},{3,7},{4,8},{5,9},{6,10},{7,11},{8,12},{9,13},{1... | collective-permute-start | bytes 786440 | tf_op jit(solution)/shard_map/ppermute | solution.py:27
  44.6 11.8 %collective-permute-start.9 = (bf16[128,1024]{1,0:T(8,128)(2,1)S(1)}, bf16[128,1024]{1,0:T(8,128)(2,1)S(1)}, u32[]{:S(2)}, u32[]{:S(2)}) collective-permute-start(bf16[128,1024]{1,0:T(8,128)(2,1)S(1)} %get-tuple-element.56), channel_id=1, source_target_pairs={{0,4},{1,5},{2,6},{3,7},{4,8},{5,9},{6,10},{7,11},{8,12},{9,13},{1... | collective-permute-start | bytes 786440 | tf_op jit(solution)/shard_map/ppermute | solution.py:27
  47.1 7.9 %collective-permute-start.10 = (bf16[128,512]{1,0:T(8,128)(2,1)S(1)}, bf16[128,512]{1,0:T(8,128)(2,1)S(1)}, u32[]{:S(2)}, u32[]{:S(2)}) collective-permute-start(bf16[128,512]{1,0:T(8,128)(2,1)S(1)} %get-tuple-element.57), channel_id=1, source_target_pairs={{0,1},{1,0},{2,3},{3,2},{4,5},{5,4},{6,7},{7,6},{8,9},{9,8},{10,11... | collective-permute-start | bytes 393224 | tf_op jit(solution)/shard_map/ppermute | solution.py:30
  47.2 7.9 %collective-permute-start.11 = (bf16[128,512]{1,0:T(8,128)(2,1)S(1)}, bf16[128,512]{1,0:T(8,128)(2,1)S(1)}, u32[]{:S(2)}, u32[]{:S(2)}) collective-permute-start(bf16[128,512]{1,0:T(8,128)(2,1)S(1)} %get-tuple-element.58), channel_id=1, source_target_pairs={{0,2},{1,3},{2,0},{3,1},{4,6},{5,7},{6,4},{7,5},{8,10},{9,11},{10,... | collective-permute-start | bytes 393224 | tf_op jit(solution)/shard_map/ppermute | solution.py:31
  53.6 11.2 %collective-permute-start.30 = (bf16[128,1024]{1,0:T(8,128)(2,1)S(1)}, bf16[128,1024]{1,0:T(8,128)(2,1)S(1)}, u32[]{:S(2)}, u32[]{:S(2)}) collective-permute-start(bf16[128,1024]{1,0:T(8,128)(2,1)S(1)} %get-tuple-element.77), channel_id=1, source_target_pairs={{0,4},{1,5},{2,6},{3,7},{4,8},{5,9},{6,10},{7,11},{8,12},{9,13},{1... | collective-permute-start | bytes 786440 | tf_op jit(solution)/shard_map/ppermute | solution.py:27
  58.1 11.7 %collective-permute-start.12 = (bf16[128,1024]{1,0:T(8,128)(2,1)S(1)}, bf16[128,1024]{1,0:T(8,128)(2,1)S(1)}, u32[]{:S(2)}, u32[]{:S(2)}) collective-permute-start(bf16[128,1024]{1,0:T(8,128)(2,1)S(1)} %get-tuple-element.59), channel_id=1, source_target_pairs={{0,4},{1,5},{2,6},{3,7},{4,8},{5,9},{6,10},{7,11},{8,12},{9,13},{1... | collective-permute-start | bytes 786440 | tf_op jit(solution)/shard_map/ppermute | solution.py:27
  60.4 9.3 %collective-permute-start.13 = (bf16[128,512]{1,0:T(8,128)(2,1)S(1)}, bf16[128,512]{1,0:T(8,128)(2,1)S(1)}, u32[]{:S(2)}, u32[]{:S(2)}) collective-permute-start(bf16[128,512]{1,0:T(8,128)(2,1)S(1)} %get-tuple-element.60), channel_id=1, source_target_pairs={{0,1},{1,0},{2,3},{3,2},{4,5},{5,4},{6,7},{7,6},{8,9},{9,8},{10,11... | collective-permute-start | bytes 393224 | tf_op jit(solution)/shard_map/ppermute | solution.py:30
  60.4 9.3 %collective-permute-start.14 = (bf16[128,512]{1,0:T(8,128)(2,1)S(1)}, bf16[128,512]{1,0:T(8,128)(2,1)S(1)}, u32[]{:S(2)}, u32[]{:S(2)}) collective-permute-start(bf16[128,512]{1,0:T(8,128)(2,1)S(1)} %get-tuple-element.61), channel_id=1, source_target_pairs={{0,2},{1,3},{2,0},{3,1},{4,6},{5,7},{6,4},{7,5},{8,10},{9,11},{10,... | collective-permute-start | bytes 393224 | tf_op jit(solution)/shard_map/ppermute | solution.py:31
  66.5 9.3 %collective-permute-start.34 = (bf16[128,512]{1,0:T(8,128)(2,1)S(1)}, bf16[128,512]{1,0:T(8,128)(2,1)S(1)}, u32[]{:S(2)}, u32[]{:S(2)}) collective-permute-start(bf16[128,512]{1,0:T(8,128)(2,1)S(1)} %get-tuple-element.81), channel_id=1, source_target_pairs={{0,1},{1,0},{2,3},{3,2},{4,5},{5,4},{6,7},{7,6},{8,9},{9,8},{10,11... | collective-permute-start | bytes 393224 | tf_op jit(solution)/shard_map/ppermute | solution.py:30
  66.6 13.5 %collective-permute-start.33 = (bf16[128,1024]{1,0:T(8,128)(2,1)S(1)}, bf16[128,1024]{1,0:T(8,128)(2,1)S(1)}, u32[]{:S(2)}, u32[]{:S(2)}) collective-permute-start(bf16[128,1024]{1,0:T(8,128)(2,1)S(1)} %get-tuple-element.80), channel_id=1, source_target_pairs={{0,4},{1,5},{2,6},{3,7},{4,8},{5,9},{6,10},{7,11},{8,12},{9,13},{1... | collective-permute-start | bytes 786440 | tf_op jit(solution)/shard_map/ppermute | solution.py:27
  71.5 11.0 %collective-permute-start.15 = (bf16[128,1024]{1,0:T(8,128)(2,1)S(1)}, bf16[128,1024]{1,0:T(8,128)(2,1)S(1)}, u32[]{:S(2)}, u32[]{:S(2)}) collective-permute-start(bf16[128,1024]{1,0:T(8,128)(2,1)S(1)} %get-tuple-element.62), channel_id=1, source_target_pairs={{0,4},{1,5},{2,6},{3,7},{4,8},{5,9},{6,10},{7,11},{8,12},{9,13},{1... | collective-permute-start | bytes 786440 | tf_op jit(solution)/shard_map/ppermute | solution.py:27
  (14 other events, 96.1 us)
where the time goes:
time: 85.2 us; the launch traced here: 85 us
  starting transfers between devices  31.9 us (37%)
  Pallas kernels  26.4 us (31%)
  waiting for transfers between devices  26.3 us (31%)
    ppermute x12, waiting for transfers between devices, exchange(): got_far = lax.ppermute(far, 'bay', [(i, i ^ 2) for i in range(count)])  20.7 us
    ppermute x12, starting transfers between devices, exchange(): lax.ppermute(onward, 'bay', [(i, (i + STRIPS) % count) for i in range(sto...  18.5 us
    pallas_call x10, Pallas kernels, step(): pl.pallas_call(functools.partial(step_body, tick, chunk), out_shape=tuple...  16.9 us
    ppermute x12, starting transfers between devices, exchange(): got_far = lax.ppermute(far, 'bay', [(i, i ^ 2) for i in range(count)])  13.3 us
    ppermute x12, waiting for transfers between devices, exchange(): lax.ppermute(onward, 'bay', [(i, (i + STRIPS) % count) for i in range(sto...  5.54 us
    pallas_call x2, Pallas kernels, last_step(): pl.pallas_call(functools.partial(last_body, tick, chunk), out_shape=jax.S...  4.77 us
    pallas_call x1, Pallas kernels, load(): pl.pallas_call(functools.partial(load_body, spans), out_shape=tuple(shape...  3.42 us
  transfers between devices with their start and end apart: 36, of which 10 were waited for; matrix products, arithmetic and copies ran while one was open for 0% of the time, Pallas kernels for 27%

commit v1 on v0

--- a/solution.py
+++ b/solution.py
@@ -13,6 +13,8 @@
 CHUNKS = 2
 COLS = 512
 EARLY = 6
+PARTS = 8
+SPARE = 0
 LIMIT = 16 << 20
 
 
@@ -103,32 +105,41 @@
     )(*in_hbm(order, traces, operator, loads))
 
 
-def prepared(tick, chunk, onward, select, seeds, patches, table):
-    size = onward.shape[0]
+def permuted(onward, select):
+    return jnp.dot(onward[...], select[...], preferred_element_type=jnp.float32).astype(
+        jnp.bfloat16
+    )
+
+
+def amplitudes(tick, chunk, size, seeds, patches, table):
     own = slice(chunk * size, (chunk + 1) * size)
-    mapped = jnp.dot(onward[...], select[...], preferred_element_type=jnp.float32).astype(
-        jnp.bfloat16
-    )
     amplitude = ((seeds[:, own] * 7 + 13 * tick) % 97 - 48).astype(jnp.float32) / 32.0
     rows = lax.broadcasted_iota(jnp.int32, (table.shape[0], size), 0)
-    loaded = jnp.where(rows == patches[:, own], amplitude, 0.0).astype(jnp.bfloat16)
-    return mapped, loaded
-
-
-def block(mapped, loaded, near, far, weights, table, low, high):
-    first = mapped.shape[1]
-    second = first + near.shape[1]
-    total = jnp.dot(near[...], weights[first:second, low:high], preferred_element_type=jnp.float32)
-    total += jnp.dot(far[...], weights[second:, low:high], preferred_element_type=jnp.float32)
+    return jnp.where(rows == patches[:, own], amplitude, 0.0).astype(jnp.bfloat16)
+
+
+def lateral(loaded, near, far, weights, table, low, high):
+    split = weights.shape[0] - far.shape[1]
+    start = split - near.shape[1]
+    total = jnp.dot(near[...], weights[start:split, low:high], preferred_element_type=jnp.float32)
+    total += jnp.dot(far[...], weights[split:, low:high], preferred_element_type=jnp.float32)
     total += lax.dot_general(
         loaded, table[:, low:high], (((0,), (0,)), ((), ())), preferred_element_type=jnp.float32
     )
-    total += jnp.dot(mapped, weights[:first, low:high], preferred_element_type=jnp.float32)
+    return total
+
+
+def block(mapped, loaded, near, far, weights, table, low, high):
+    total = lateral(loaded, near, far, weights, table, low, high)
+    total += jnp.dot(
+        mapped, weights[: mapped.shape[1], low:high], preferred_element_type=jnp.float32
+    )
     return total.astype(jnp.bfloat16)
 
 
 def step_body(tick, chunk, onward, near, far, select, seeds, patches, table, weights, *outs):
-    mapped, loaded = prepared(tick, chunk, onward, select, seeds, patches, table)
+    mapped = permuted(onward, select)
+    loaded = amplitudes(tick, chunk, onward.shape[0], seeds, patches, table)
     start = 0
     for out in outs:
         for low in range(0, out.shape[1], COLS):
@@ -138,6 +149,36 @@
         start += out.shape[1]
 
 
+def late_body(tick, chunk, parts, onward, near, far, seeds, patches, table, weights, *refs):
+    uppers, outs = refs[:parts], refs[parts:]
+    loaded = amplitudes(tick, chunk, onward.shape[0], seeds, patches, table)
+    low, start = 0, 0
+    ends = []
+    for out in outs:
+        start += out.shape[1]
+        ends.append(start)
+    for upper in uppers:
+        high = low + upper.shape[1]
+        total = lateral(loaded, near, far, weights, table, low, high)
+        total += jnp.dot(onward[...], upper[...], preferred_element_type=jnp.float32)
+        for out, end in zip(outs, ends):
+            begin = end - out.shape[1]
+            if begin <= low < end:
+                out[:, low - begin : high - begin] = total.astype(jnp.bfloat16)
+        low = high
+
+
+def late_step(tick, chunk, got, common, weights, uppers):
+    return pl.pallas_call(
+        functools.partial(late_body, tick, chunk, len(uppers)),
+        out_shape=tuple(jax.ShapeDtypeStruct(piece.shape, jnp.bfloat16) for piece in got),
+        in_specs=[VMEM] * (len(uppers) + 7),
+        out_specs=(VMEM,) * 3,
+        compiler_params=pltpu.CompilerParams(vmem_limit_bytes=LIMIT),
+        cost_estimate=cost(got[0].shape[0], weights),
+    )(*got, *common[1:], weights, *uppers)
+
+
 def cost(rows, weights):
     return pl.CostEstimate(
         flops=2 * rows * weights.shape[0] * weights.shape[1],
@@ -157,44 +198,90 @@
     )(*got, *common, weights)
 
 
-def last_body(tick, chunk, onward, near, far, select, seeds, patches, table, weights, *rest):
-    out, buffer, sems = rest[-3:]
-    rows, width = buffer.shape
-    mapped, loaded = prepared(tick, chunk, onward, select, seeds, patches, table)
+def column_body(low, select, weights, out):
+    out[...] = jnp.dot(
+        select[...],
+        weights[: select.shape[1], low : low + out.shape[1]],
+        preferred_element_type=jnp.float32,
+    ).astype(jnp.bfloat16)
+
+
+def columns_of(low, width, select, weights):
+    size = select.shape[0]
+    return pl.pallas_call(
+        functools.partial(column_body, low),
+        out_shape=jax.ShapeDtypeStruct((size, width), jnp.bfloat16),
+        in_specs=[VMEM] * 2,
+        out_specs=VMEM,
+        name="columns",
+        compiler_params=pltpu.CompilerParams(vmem_limit_bytes=LIMIT),
+        cost_estimate=pl.CostEstimate(
+            flops=2 * size * size * width, transcendentals=0, bytes_accessed=size * size * 2
+        ),
+    )(select, weights)
+
+
+def side_body(tick, chunk, near, far, seeds, patches, table, weights, out):
+    loaded = amplitudes(tick, chunk, near.shape[0], seeds, patches, table)
+    for low in range(0, out.shape[1], COLS):
+        out[:, low : low + COLS] = lateral(loaded, near, far, weights, table, low, low + COLS)
+
+
+def side(tick, chunk, got, common, weights):
+    return pl.pallas_call(
+        functools.partial(side_body, tick, chunk),
+        out_shape=jax.ShapeDtypeStruct((got[0].shape[0], weights.shape[1]), jnp.float32),
+        in_specs=[VMEM] * 6,
+        out_specs=VMEM,
+        name="side",
+        compiler_params=pltpu.CompilerParams(vmem_limit_bytes=LIMIT),
+        cost_estimate=cost(got[0].shape[0] // 2, weights),
+    )(*got[1:], *common[1:], weights)
+
+
+def last_body(chunk, parts, onward, beside, *refs):
+    uppers = refs[:parts]
+    out, buffer, sems = refs[-3:]
+    rows = buffer.shape[0]
     copies = []
-    for index, low in enumerate(range(0, width, COLS)):
-        buffer[:, low : low + COLS] = block(
-            mapped, loaded, near, far, weights, table, low, low + COLS
+    low = 0
+    for index, upper in enumerate(uppers):
+        high = low + upper.shape[1]
+        total = beside[:, low:high] + jnp.dot(
+            onward[...], upper[...], preferred_element_type=jnp.float32
         )
+        buffer[:, low:high] = total.astype(jnp.bfloat16)
         copies.append(
             pltpu.make_async_copy(
-                buffer.at[:, low : low + COLS],
-                out.at[0, chunk * rows : (chunk + 1) * rows, low : low + COLS],
+                buffer.at[:, low:high],
+                out.at[0, chunk * rows : (chunk + 1) * rows, low:high],
                 sems.at[index],
             )
         )
         copies[-1].start()
+        low = high
     for copy in copies:
         copy.wait()
 
 
-def last_step(tick, chunk, got, common, weights, previous):
+def last_step(tick, chunk, got, common, weights, uppers, previous):
     rows, width = got[0].shape[0], weights.shape[1]
     extra = [] if previous is None else [previous]
-    return pl.pallas_call(
-        functools.partial(last_body, tick, chunk),
+    beside = side(tick, chunk, got, common, weights)
+    return pl.pallas_call(
+        functools.partial(last_body, chunk, len(uppers)),
         out_shape=jax.ShapeDtypeStruct((1, rows * CHUNKS, width), jnp.bfloat16),
-        in_specs=[VMEM] * 8 + [ANY] * len(extra),
+        in_specs=[VMEM] * (len(uppers) + 2) + [ANY] * len(extra),
         out_specs=ANY,
         scratch_shapes=[
             pltpu.VMEM((rows, width), jnp.bfloat16),
-            pltpu.SemaphoreType.DMA((pl.cdiv(width, COLS),)),
+            pltpu.SemaphoreType.DMA((len(uppers),)),
         ],
-        input_output_aliases={8: 0} if extra else {},
+        input_output_aliases={len(uppers) + 2: 0} if extra else {},
         name="last",
         compiler_params=pltpu.CompilerParams(vmem_limit_bytes=LIMIT),
-        cost_estimate=cost(rows, weights),
-    )(*got, *common, weights, *extra)
+        cost_estimate=cost(rows // 2, weights),
+    )(got[0], beside, *uppers, *extra)
 
 
 def on_device(traces, operator, loads, seeds, patches, trace_map):
@@ -217,14 +304,21 @@
         got.append(exchange(pieces[3 * c : 3 * c + 3], count))
 
     common = (select, seeds[None], patches, table)
+    uppers = []
     out = None
     for tick in range(TICKS):
         for c in range(CHUNKS):
             if tick == TICKS - 1:
-                out = last_step(tick, c, got[c], common, weights, out)
+                out = last_step(tick, c, got[c], common, weights, uppers, out)
             else:
-                pieces = step(tick, c, got[c], common, weights)
-                got[c] = exchange(pieces, count, tick + 2 < TICKS)
+                if len(uppers) == PARTS:
+                    pieces = late_step(tick, c, got[c], common, weights, uppers)
+                else:
+                    pieces = step(tick, c, got[c], common, weights)
+                if SPARE <= CHUNKS * tick + c < SPARE + PARTS:
+                    part = width // PARTS
+                    uppers.append(columns_of(len(uppers) * part, part, select, weights))
+                got[c] = exchange(pieces, count, (tick, c) != (TICKS - 2, CHUNKS - 1))
     return out
 
 

time: 85.2 us -> 87 us (1.021)
  Pallas kernels: 26.4 us -> 31.4 us
  waiting for transfers between devices: 26.3 us -> 21.3 us
  starting transfers between devices: 31.9 us -> 33.7 us
    pallas_call x2 -> x14, Pallas kernels: 4.77 us -> 13.1 us  [the longest x8 5.71 us: columns_of(): pl.pallas_call(functools.partial(column_body, low), out_shape=jax.ShapeDt...]
    ppermute x12, waiting for transfers between devices: 20.7 us -> 15.7 us  [exchange(): got_far = lax.ppermute(far, 'bay', [(i, i ^ 2) for i in range(count)])]
    pallas_call x10 -> x8, Pallas kernels: 16.9 us -> 13.6 us  [step(): pl.pallas_call(functools.partial(step_body, tick, chunk), out_shape=tuple...]
    ppermute x12, starting transfers between devices: 13.3 us -> 14.9 us  [exchange(): got_far = lax.ppermute(far, 'bay', [(i, i ^ 2) for i in range(count)])]
  transfers between devices with their start and end apart: 36 -> 36, of which waited for: 10 -> 10; matrix products, arithmetic and copies ran while one was open for 0% -> 0% of each run, Pallas kernels for 27% -> 33%
where the time goes in v1:
time: 87 us; the launch traced here: 86.8 us
  starting transfers between devices  33.7 us (39%)
  Pallas kernels  31.4 us (36%)
  waiting for transfers between devices  21.3 us (24%)
    ppermute x12, starting transfers between devices, exchange(): lax.ppermute(onward, 'bay', [(i, (i + STRIPS) % count) for i in range(sto...  17.9 us
    ppermute x12, waiting for transfers between devices, exchange(): got_far = lax.ppermute(far, 'bay', [(i, i ^ 2) for i in range(count)])  15.7 us
    ppermute x12, starting transfers between devices, exchange(): got_far = lax.ppermute(far, 'bay', [(i, i ^ 2) for i in range(count)])  14.9 us
    pallas_call x8, Pallas kernels, step(): pl.pallas_call(functools.partial(step_body, tick, chunk), out_shape=tuple...  13.6 us
    pallas_call x8, Pallas kernels, columns_of(): pl.pallas_call(functools.partial(column_body, low), out_shape=jax.ShapeDt...  5.71 us
    ppermute x12, waiting for transfers between devices, exchange(): lax.ppermute(onward, 'bay', [(i, (i + STRIPS) % count) for i in range(sto...  5.5 us
    pallas_call x1, Pallas kernels, load(): pl.pallas_call(functools.partial(load_body, spans), out_shape=tuple(shape...  3.42 us
    pallas_call x2, Pallas kernels, last_step(): pl.pallas_call(functools.partial(last_body, chunk, len(uppers)), out_shap...  2.9 us
  transfers between devices with their start and end apart: 36, of which 10 were waited for; matrix products, arithmetic and copies ran while one was open for 0% of the time, Pallas kernels for 33%

profile of v1, /device:TPU:0, one launch (start us, length us, event | category | flops | bytes accessed | tf_op | source)
XLA Modules:
  0.0 86.8 jit_solution(12937685225261050338)
XLA Ops:
  1.3 3.1 %collective-permute-start.18 = (bf16[128,1024]{1,0:T(8,128)(2,1)S(1)}, bf16[128,1024]{1,0:T(8,128)(2,1)S(1)}, u32[]{:S(2)}, u32[]{:S(2)}) collective-permute-start(bf16[128,1024]{1,0:T(8,128)(2,1)S(1)} %get-tuple-element.65), channel_id=1, source_target_pairs={{0,4},{1,5},{2,6},{3,7},{4,8},{5,9},{6,10},{7,11},{8,12},{9,13},{1... | collective-permute-start | bytes 786440 | tf_op jit(solution)/shard_map/ppermute | solution.py:29
  4.4 1.6 %collective-permute-start = (bf16[128,1024]{1,0:T(8,128)(2,1)S(1)}, bf16[128,1024]{1,0:T(8,128)(2,1)S(1)}, u32[]{:S(2)}, u32[]{:S(2)}) collective-permute-start(bf16[128,1024]{1,0:T(8,128)(2,1)S(1)} %get-tuple-element.44), channel_id=1, source_target_pairs={{0,4},{1,5},{2,6},{3,7},{4,8},{5,9},{6,10},{7,11},{8,12},{9,13},{1... | collective-permute-start | bytes 786440 | tf_op jit(solution)/shard_map/ppermute | solution.py:29
  8.0 3.4 %load.1 = (bf16[1024,1024]{1,0:T(8,128)(2,1)S(1)}, bf16[2048,2048]{1,0:T(8,128)(2,1)S(1)}, bf16[16,2048]{1,0:T(8,128)(2,1)S(1)}) custom-call(s32[1,1024]{1,0:T(1,128)} %trace_map.1, bf16[1,256,2048]{2,1,0:T(8,128)(2,1)} %source.3, bf16[1,2048,2048]{2,1,0:T(8,128)(2,1)} %operator.1, bf16[1,16,2048]{2,1,0:T(8,128)(2,1)} %table.1), custom_call_target="tpu_custom_call" | custom-call | tf_op jit(solution)/shard_map/load/pallas_call | solution.py:94
  13.6 1.7 %shard_map.69 = (bf16[128,1024]{1,0:T(8,128)(2,1)S(1)}, bf16[128,512]{1,0:T(8,128)(2,1)S(1)}, bf16[128,512]{1,0:T(8,128)(2,1)S(1)}) custom-call(bf16[128,1024]{1,0:T(8,128)(2,1)S(1)} %collective-permute-done.18.onward, bf16[128,512]{1,0:T(8,128)(2,1)S(1)} %collective-permute-done.19.near, bf16[128,512]{1,0:T(8,128)(2,1)S(1)} %collective-permute-done.20.far, ...), custom_call_target="tpu_custom_call" | custom-call | flops 1073741824 | bytes 8388608 | tf_op jit(solution)/shard_map/pallas_call | solution.py:191
  15.7 2.8 %collective-permute-done.onward = bf16[128,1024]{1,0:T(8,128)(2,1)S(1)} collective-permute-done((bf16[128,1024]{1,0:T(8,128)(2,1)S(1)}, bf16[128,1024]{1,0:T(8,128)(2,1)S(1)}, u32[]{:S(2)}, u32[]{:S(2)}) %collective-permute-start) | collective-permute-done | bytes 262176 | tf_op jit(solution)/shard_map/ppermute | solution.py:29
  18.6 1.7 %shard_map.64 = (bf16[128,1024]{1,0:T(8,128)(2,1)S(1)}, bf16[128,512]{1,0:T(8,128)(2,1)S(1)}, bf16[128,512]{1,0:T(8,128)(2,1)S(1)}) custom-call(bf16[128,1024]{1,0:T(8,128)(2,1)S(1)} %collective-permute-done.onward, bf16[128,512]{1,0:T(8,128)(2,1)S(1)} %collective-permute-done.1.near, bf16[128,512]{1,0:T(8,128)(2,1)S(1)} %collective-permute-done.2.far, ...), custom_call_target="tpu_custom_call" | custom-call | flops 1073741824 | bytes 8388608 | tf_op jit(solution)/shard_map/pallas_call | solution.py:191
  20.3 1.8 %collective-permute-start.23 = (bf16[128,512]{1,0:T(8,128)(2,1)S(1)}, bf16[128,512]{1,0:T(8,128)(2,1)S(1)}, u32[]{:S(2)}, u32[]{:S(2)}) collective-permute-start(bf16[128,512]{1,0:T(8,128)(2,1)S(1)} %get-tuple-element.70), channel_id=1, source_target_pairs={{0,2},{1,3},{2,0},{3,1},{4,6},{5,7},{6,4},{7,5},{8,10},{9,11},{10,... | collective-permute-start | bytes 393224 | tf_op jit(solution)/shard_map/ppermute | solution.py:33
  22.4 3.4 %collective-permute-done.23.far = bf16[128,512]{1,0:T(8,128)(2,1)S(1)} collective-permute-done((bf16[128,512]{1,0:T(8,128)(2,1)S(1)}, bf16[128,512]{1,0:T(8,128)(2,1)S(1)}, u32[]{:S(2)}, u32[]{:S(2)}) %collective-permute-start.23) | collective-permute-done | bytes 131104 | tf_op jit(solution)/shard_map/ppermute | solution.py:33
  25.9 1.7 %shard_map.70 = (bf16[128,1024]{1,0:T(8,128)(2,1)S(1)}, bf16[128,512]{1,0:T(8,128)(2,1)S(1)}, bf16[128,512]{1,0:T(8,128)(2,1)S(1)}) custom-call(bf16[128,1024]{1,0:T(8,128)(2,1)S(1)} %collective-permute-done.21.onward, bf16[128,512]{1,0:T(8,128)(2,1)S(1)} %collective-permute-done.22.near, bf16[128,512]{1,0:T(8,128)(2,1)S(1)} %collective-permute-done.23.far, ...), custom_call_target="tpu_custom_call" | custom-call | flops 1073741824 | bytes 8388608 | tf_op jit(solution)/shard_map/pallas_call | solution.py:191
  27.7 2.1 %collective-permute-start.24 = (bf16[128,1024]{1,0:T(8,128)(2,1)S(1)}, bf16[128,1024]{1,0:T(8,128)(2,1)S(1)}, u32[]{:S(2)}, u32[]{:S(2)}) collective-permute-start(bf16[128,1024]{1,0:T(8,128)(2,1)S(1)} %get-tuple-element.71), channel_id=1, source_target_pairs={{0,4},{1,5},{2,6},{3,7},{4,8},{5,9},{6,10},{7,11},{8,12},{9,13},{1... | collective-permute-start | bytes 786440 | tf_op jit(solution)/shard_map/ppermute | solution.py:29
  29.8 1.7 %shard_map.65 = (bf16[128,1024]{1,0:T(8,128)(2,1)S(1)}, bf16[128,512]{1,0:T(8,128)(2,1)S(1)}, bf16[128,512]{1,0:T(8,128)(2,1)S(1)}) custom-call(bf16[128,1024]{1,0:T(8,128)(2,1)S(1)} %collective-permute-done.3.onward, bf16[128,512]{1,0:T(8,128)(2,1)S(1)} %collective-permute-done.4.near, bf16[128,512]{1,0:T(8,128)(2,1)S(1)} %collective-permute-done.5.far, ...), custom_call_target="tpu_custom_call" | custom-call | flops 1073741824 | bytes 8388608 | tf_op jit(solution)/shard_map/pallas_call | solution.py:191
  31.5 1.6 %collective-permute-start.6 = (bf16[128,1024]{1,0:T(8,128)(2,1)S(1)}, bf16[128,1024]{1,0:T(8,128)(2,1)S(1)}, u32[]{:S(2)}, u32[]{:S(2)}) collective-permute-start(bf16[128,1024]{1,0:T(8,128)(2,1)S(1)} %get-tuple-element.53), channel_id=1, source_target_pairs={{0,4},{1,5},{2,6},{3,7},{4,8},{5,9},{6,10},{7,11},{8,12},{9,13},{1... | collective-permute-start | bytes 786440 | tf_op jit(solution)/shard_map/ppermute | solution.py:29
  33.1 2.5 %collective-permute-start.26 = (bf16[128,512]{1,0:T(8,128)(2,1)S(1)}, bf16[128,512]{1,0:T(8,128)(2,1)S(1)}, u32[]{:S(2)}, u32[]{:S(2)}) collective-permute-start(bf16[128,512]{1,0:T(8,128)(2,1)S(1)} %get-tuple-element.73), channel_id=1, source_target_pairs={{0,2},{1,3},{2,0},{3,1},{4,6},{5,7},{6,4},{7,5},{8,10},{9,11},{10,... | collective-permute-start | bytes 393224 | tf_op jit(solution)/shard_map/ppermute | solution.py:33
  35.6 3.9 %collective-permute-done.26.far = bf16[128,512]{1,0:T(8,128)(2,1)S(1)} collective-permute-done((bf16[128,512]{1,0:T(8,128)(2,1)S(1)}, bf16[128,512]{1,0:T(8,128)(2,1)S(1)}, u32[]{:S(2)}, u32[]{:S(2)}) %collective-permute-start.26) | collective-permute-done | bytes 131104 | tf_op jit(solution)/shard_map/ppermute | solution.py:33
  39.5 1.7 %shard_map.71 = (bf16[128,1024]{1,0:T(8,128)(2,1)S(1)}, bf16[128,512]{1,0:T(8,128)(2,1)S(1)}, bf16[128,512]{1,0:T(8,128)(2,1)S(1)}) custom-call(bf16[128,1024]{1,0:T(8,128)(2,1)S(1)} %collective-permute-done.24.onward, bf16[128,512]{1,0:T(8,128)(2,1)S(1)} %collective-permute-done.25.near, bf16[128,512]{1,0:T(8,128)(2,1)S(1)} %collective-permute-done.26.far, ...), custom_call_target="tpu_custom_call" | custom-call | flops 1073741824 | bytes 8388608 | tf_op jit(solution)/shard_map/pallas_call | solution.py:191
  44.0 1.7 %shard_map.66 = (bf16[128,1024]{1,0:T(8,128)(2,1)S(1)}, bf16[128,512]{1,0:T(8,128)(2,1)S(1)}, bf16[128,512]{1,0:T(8,128)(2,1)S(1)}) custom-call(bf16[128,1024]{1,0:T(8,128)(2,1)S(1)} %collective-permute-done.6.onward, bf16[128,512]{1,0:T(8,128)(2,1)S(1)} %collective-permute-done.7.near, bf16[128,512]{1,0:T(8,128)(2,1)S(1)} %collective-permute-done.8.far, ...), custom_call_target="tpu_custom_call" | custom-call | flops 1073741824 | bytes 8388608 | tf_op jit(solution)/shard_map/pallas_call | solution.py:191
  46.7 3.0 %collective-permute-start.29 = (bf16[128,512]{1,0:T(8,128)(2,1)S(1)}, bf16[128,512]{1,0:T(8,128)(2,1)S(1)}, u32[]{:S(2)}, u32[]{:S(2)}) collective-permute-start(bf16[128,512]{1,0:T(8,128)(2,1)S(1)} %get-tuple-element.76), channel_id=1, source_target_pairs={{0,2},{1,3},{2,0},{3,1},{4,6},{5,7},{6,4},{7,5},{8,10},{9,11},{10,... | collective-permute-start | bytes 393224 | tf_op jit(solution)/shard_map/ppermute | solution.py:33
  53.9 1.7 %shard_map.72 = (bf16[128,1024]{1,0:T(8,128)(2,1)S(1)}, bf16[128,512]{1,0:T(8,128)(2,1)S(1)}, bf16[128,512]{1,0:T(8,128)(2,1)S(1)}) custom-call(bf16[128,1024]{1,0:T(8,128)(2,1)S(1)} %collective-permute-done.27.onward, bf16[128,512]{1,0:T(8,128)(2,1)S(1)} %collective-permute-done.28.near, bf16[128,512]{1,0:T(8,128)(2,1)S(1)} %collective-permute-done.29.far, ...), custom_call_target="tpu_custom_call" | custom-call | flops 1073741824 | bytes 8388608 | tf_op jit(solution)/shard_map/pallas_call | solution.py:191
  55.6 1.6 %collective-permute-start.30 = (bf16[128,1024]{1,0:T(8,128)(2,1)S(1)}, bf16[128,1024]{1,0:T(8,128)(2,1)S(1)}, u32[]{:S(2)}, u32[]{:S(2)}) collective-permute-start(bf16[128,1024]{1,0:T(8,128)(2,1)S(1)} %get-tuple-element.77), channel_id=1, source_target_pairs={{0,4},{1,5},{2,6},{3,7},{4,8},{5,9},{6,10},{7,11},{8,12},{9,13},{1... | collective-permute-start | bytes 786440 | tf_op jit(solution)/shard_map/ppermute | solution.py:29
  57.2 1.7 %shard_map.67 = (bf16[128,1024]{1,0:T(8,128)(2,1)S(1)}, bf16[128,512]{1,0:T(8,128)(2,1)S(1)}, bf16[128,512]{1,0:T(8,128)(2,1)S(1)}) custom-call(bf16[128,1024]{1,0:T(8,128)(2,1)S(1)} %collective-permute-done.9.onward, bf16[128,512]{1,0:T(8,128)(2,1)S(1)} %collective-permute-done.10.near, bf16[128,512]{1,0:T(8,128)(2,1)S(1)} %collective-permute-done.11.far, ...), custom_call_target="tpu_custom_call" | custom-call | flops 1073741824 | bytes 8388608 | tf_op jit(solution)/shard_map/pallas_call | solution.py:191
  61.2 2.1 %collective-permute-start.32 = (bf16[128,512]{1,0:T(8,128)(2,1)S(1)}, bf16[128,512]{1,0:T(8,128)(2,1)S(1)}, u32[]{:S(2)}, u32[]{:S(2)}) collective-permute-start(bf16[128,512]{1,0:T(8,128)(2,1)S(1)} %get-tuple-element.79), channel_id=1, source_target_pairs={{0,2},{1,3},{2,0},{3,1},{4,6},{5,7},{6,4},{7,5},{8,10},{9,11},{10,... | collective-permute-start | bytes 393224 | tf_op jit(solution)/shard_map/ppermute | solution.py:33
  68.9 2.3 %collective-permute-start.35 = (bf16[128,512]{1,0:T(8,128)(2,1)S(1)}, bf16[128,512]{1,0:T(8,128)(2,1)S(1)}, u32[]{:S(2)}, u32[]{:S(2)}) collective-permute-start(bf16[128,512]{1,0:T(8,128)(2,1)S(1)} %get-tuple-element.82), channel_id=1, source_target_pairs={{0,2},{1,3},{2,0},{3,1},{4,6},{5,7},{6,4},{7,5},{8,10},{9,11},{10,... | collective-permute-start | bytes 393224 | tf_op jit(solution)/shard_map/ppermute | solution.py:33
  74.2 2.7 %collective-permute-start.15 = (bf16[128,1024]{1,0:T(8,128)(2,1)S(1)}, bf16[128,1024]{1,0:T(8,128)(2,1)S(1)}, u32[]{:S(2)}, u32[]{:S(2)}) collective-permute-start(bf16[128,1024]{1,0:T(8,128)(2,1)S(1)} %get-tuple-element.62), channel_id=1, source_target_pairs={{0,4},{1,5},{2,6},{3,7},{4,8},{5,9},{6,10},{7,11},{8,12},{9,13},{1... | collective-permute-start | bytes 786440 | tf_op jit(solution)/shard_map/ppermute | solution.py:29
  78.3 4.6 %collective-permute-done.17.far = bf16[128,512]{1,0:T(8,128)(2,1)S(1)} collective-permute-done((bf16[128,512]{1,0:T(8,128)(2,1)S(1)}, bf16[128,512]{1,0:T(8,128)(2,1)S(1)}, u32[]{:S(2)}, u32[]{:S(2)}) %collective-permute-start.17) | collective-permute-done | bytes 131104 | tf_op jit(solution)/shard_map/ppermute | solution.py:33
  (76 shorter events, 30.3 us)
Async XLA Ops:
  1.3 12.3 %collective-permute-start.18 = (bf16[128,1024]{1,0:T(8,128)(2,1)S(1)}, bf16[128,1024]{1,0:T(8,128)(2,1)S(1)}, u32[]{:S(2)}, u32[]{:S(2)}) collective-permute-start(bf16[128,1024]{1,0:T(8,128)(2,1)S(1)} %get-tuple-element.65), channel_id=1, source_target_pairs={{0,4},{1,5},{2,6},{3,7},{4,8},{5,9},{6,10},{7,11},{8,12},{9,13},{1... | collective-permute-start | bytes 786440 | tf_op jit(solution)/shard_map/ppermute | solution.py:29
  4.4 14.1 %collective-permute-start = (bf16[128,1024]{1,0:T(8,128)(2,1)S(1)}, bf16[128,1024]{1,0:T(8,128)(2,1)S(1)}, u32[]{:S(2)}, u32[]{:S(2)}) collective-permute-start(bf16[128,1024]{1,0:T(8,128)(2,1)S(1)} %get-tuple-element.44), channel_id=1, source_target_pairs={{0,4},{1,5},{2,6},{3,7},{4,8},{5,9},{6,10},{7,11},{8,12},{9,13},{1... | collective-permute-start | bytes 786440 | tf_op jit(solution)/shard_map/ppermute | solution.py:29
  7.5 8.2 %collective-permute-start.1 = (bf16[128,512]{1,0:T(8,128)(2,1)S(1)}, bf16[128,512]{1,0:T(8,128)(2,1)S(1)}, u32[]{:S(2)}, u32[]{:S(2)}) collective-permute-start(bf16[128,512]{1,0:T(8,128)(2,1)S(1)} %get-tuple-element.45), channel_id=1, source_target_pairs={{0,1},{1,0},{2,3},{3,2},{4,5},{5,4},{6,7},{7,6},{8,9},{9,8},{10,11... | collective-permute-start | bytes 393224 | tf_op jit(solution)/shard_map/ppermute | solution.py:32
  7.5 8.2 %collective-permute-start.2 = (bf16[128,512]{1,0:T(8,128)(2,1)S(1)}, bf16[128,512]{1,0:T(8,128)(2,1)S(1)}, u32[]{:S(2)}, u32[]{:S(2)}) collective-permute-start(bf16[128,512]{1,0:T(8,128)(2,1)S(1)} %get-tuple-element.46), channel_id=1, source_target_pairs={{0,2},{1,3},{2,0},{3,1},{4,6},{5,7},{6,4},{7,5},{8,10},{9,11},{10,... | collective-permute-start | bytes 393224 | tf_op jit(solution)/shard_map/ppermute | solution.py:33
  15.3 10.6 %collective-permute-start.21 = (bf16[128,1024]{1,0:T(8,128)(2,1)S(1)}, bf16[128,1024]{1,0:T(8,128)(2,1)S(1)}, u32[]{:S(2)}, u32[]{:S(2)}) collective-permute-start(bf16[128,1024]{1,0:T(8,128)(2,1)S(1)} %get-tuple-element.68), channel_id=1, source_target_pairs={{0,4},{1,5},{2,6},{3,7},{4,8},{5,9},{6,10},{7,11},{8,12},{9,13},{1... | collective-permute-start | bytes 786440 | tf_op jit(solution)/shard_map/ppermute | solution.py:29
  20.3 9.5 %collective-permute-start.3 = (bf16[128,1024]{1,0:T(8,128)(2,1)S(1)}, bf16[128,1024]{1,0:T(8,128)(2,1)S(1)}, u32[]{:S(2)}, u32[]{:S(2)}) collective-permute-start(bf16[128,1024]{1,0:T(8,128)(2,1)S(1)} %get-tuple-element.50), channel_id=1, source_target_pairs={{0,4},{1,5},{2,6},{3,7},{4,8},{5,9},{6,10},{7,11},{8,12},{9,13},{1... | collective-permute-start | bytes 786440 | tf_op jit(solution)/shard_map/ppermute | solution.py:29
  22.2 7.6 %collective-permute-start.4 = (bf16[128,512]{1,0:T(8,128)(2,1)S(1)}, bf16[128,512]{1,0:T(8,128)(2,1)S(1)}, u32[]{:S(2)}, u32[]{:S(2)}) collective-permute-start(bf16[128,512]{1,0:T(8,128)(2,1)S(1)} %get-tuple-element.51), channel_id=1, source_target_pairs={{0,1},{1,0},{2,3},{3,2},{4,5},{5,4},{6,7},{7,6},{8,9},{9,8},{10,11... | collective-permute-start | bytes 393224 | tf_op jit(solution)/shard_map/ppermute | solution.py:32
  22.2 7.6 %collective-permute-start.5 = (bf16[128,512]{1,0:T(8,128)(2,1)S(1)}, bf16[128,512]{1,0:T(8,128)(2,1)S(1)}, u32[]{:S(2)}, u32[]{:S(2)}) collective-permute-start(bf16[128,512]{1,0:T(8,128)(2,1)S(1)} %get-tuple-element.52), channel_id=1, source_target_pairs={{0,2},{1,3},{2,0},{3,1},{4,6},{5,7},{6,4},{7,5},{8,10},{9,11},{10,... | collective-permute-start | bytes 393224 | tf_op jit(solution)/shard_map/ppermute | solution.py:33
  27.6 8.0 %collective-permute-start.25 = (bf16[128,512]{1,0:T(8,128)(2,1)S(1)}, bf16[128,512]{1,0:T(8,128)(2,1)S(1)}, u32[]{:S(2)}, u32[]{:S(2)}) collective-permute-start(bf16[128,512]{1,0:T(8,128)(2,1)S(1)} %get-tuple-element.72), channel_id=1, source_target_pairs={{0,1},{1,0},{2,3},{3,2},{4,5},{5,4},{6,7},{7,6},{8,9},{9,8},{10,11... | collective-permute-start | bytes 393224 | tf_op jit(solution)/shard_map/ppermute | solution.py:32
  27.7 11.9 %collective-permute-start.24 = (bf16[128,1024]{1,0:T(8,128)(2,1)S(1)}, bf16[128,1024]{1,0:T(8,128)(2,1)S(1)}, u32[]{:S(2)}, u32[]{:S(2)}) collective-permute-start(bf16[128,1024]{1,0:T(8,128)(2,1)S(1)} %get-tuple-element.71), channel_id=1, source_target_pairs={{0,4},{1,5},{2,6},{3,7},{4,8},{5,9},{6,10},{7,11},{8,12},{9,13},{1... | collective-permute-start | bytes 786440 | tf_op jit(solution)/shard_map/ppermute | solution.py:29
  31.5 12.5 %collective-permute-start.6 = (bf16[128,1024]{1,0:T(8,128)(2,1)S(1)}, bf16[128,1024]{1,0:T(8,128)(2,1)S(1)}, u32[]{:S(2)}, u32[]{:S(2)}) collective-permute-start(bf16[128,1024]{1,0:T(8,128)(2,1)S(1)} %get-tuple-element.53), channel_id=1, source_target_pairs={{0,4},{1,5},{2,6},{3,7},{4,8},{5,9},{6,10},{7,11},{8,12},{9,13},{1... | collective-permute-start | bytes 786440 | tf_op jit(solution)/shard_map/ppermute | solution.py:29
  35.6 7.0 %collective-permute-start.7 = (bf16[128,512]{1,0:T(8,128)(2,1)S(1)}, bf16[128,512]{1,0:T(8,128)(2,1)S(1)}, u32[]{:S(2)}, u32[]{:S(2)}) collective-permute-start(bf16[128,512]{1,0:T(8,128)(2,1)S(1)} %get-tuple-element.54), channel_id=1, source_target_pairs={{0,1},{1,0},{2,3},{3,2},{4,5},{5,4},{6,7},{7,6},{8,9},{9,8},{10,11... | collective-permute-start | bytes 393224 | tf_op jit(solution)/shard_map/ppermute | solution.py:32
  35.6 7.0 %collective-permute-start.8 = (bf16[128,512]{1,0:T(8,128)(2,1)S(1)}, bf16[128,512]{1,0:T(8,128)(2,1)S(1)}, u32[]{:S(2)}, u32[]{:S(2)}) collective-permute-start(bf16[128,512]{1,0:T(8,128)(2,1)S(1)} %get-tuple-element.55), channel_id=1, source_target_pairs={{0,2},{1,3},{2,0},{3,1},{4,6},{5,7},{6,4},{7,5},{8,10},{9,11},{10,... | collective-permute-start | bytes 393224 | tf_op jit(solution)/shard_map/ppermute | solution.py:33
  41.2 12.7 %collective-permute-start.27 = (bf16[128,1024]{1,0:T(8,128)(2,1)S(1)}, bf16[128,1024]{1,0:T(8,128)(2,1)S(1)}, u32[]{:S(2)}, u32[]{:S(2)}) collective-permute-start(bf16[128,1024]{1,0:T(8,128)(2,1)S(1)} %get-tuple-element.74), channel_id=1, source_target_pairs={{0,4},{1,5},{2,6},{3,7},{4,8},{5,9},{6,10},{7,11},{8,12},{9,13},{1... | collective-permute-start | bytes 786440 | tf_op jit(solution)/shard_map/ppermute | solution.py:29
  45.7 11.6 %collective-permute-start.9 = (bf16[128,1024]{1,0:T(8,128)(2,1)S(1)}, bf16[128,1024]{1,0:T(8,128)(2,1)S(1)}, u32[]{:S(2)}, u32[]{:S(2)}) collective-permute-start(bf16[128,1024]{1,0:T(8,128)(2,1)S(1)} %get-tuple-element.56), channel_id=1, source_target_pairs={{0,4},{1,5},{2,6},{3,7},{4,8},{5,9},{6,10},{7,11},{8,12},{9,13},{1... | collective-permute-start | bytes 786440 | tf_op jit(solution)/shard_map/ppermute | solution.py:29
  46.7 7.2 %collective-permute-start.29 = (bf16[128,512]{1,0:T(8,128)(2,1)S(1)}, bf16[128,512]{1,0:T(8,128)(2,1)S(1)}, u32[]{:S(2)}, u32[]{:S(2)}) collective-permute-start(bf16[128,512]{1,0:T(8,128)(2,1)S(1)} %get-tuple-element.76), channel_id=1, source_target_pairs={{0,2},{1,3},{2,0},{3,1},{4,6},{5,7},{6,4},{7,5},{8,10},{9,11},{10,... | collective-permute-start | bytes 393224 | tf_op jit(solution)/shard_map/ppermute | solution.py:33
  55.6 11.8 %collective-permute-start.30 = (bf16[128,1024]{1,0:T(8,128)(2,1)S(1)}, bf16[128,1024]{1,0:T(8,128)(2,1)S(1)}, u32[]{:S(2)}, u32[]{:S(2)}) collective-permute-start(bf16[128,1024]{1,0:T(8,128)(2,1)S(1)} %get-tuple-element.77), channel_id=1, source_target_pairs={{0,4},{1,5},{2,6},{3,7},{4,8},{5,9},{6,10},{7,11},{8,12},{9,13},{1... | collective-permute-start | bytes 786440 | tf_op jit(solution)/shard_map/ppermute | solution.py:29
  58.9 13.8 %collective-permute-start.12 = (bf16[128,1024]{1,0:T(8,128)(2,1)S(1)}, bf16[128,1024]{1,0:T(8,128)(2,1)S(1)}, u32[]{:S(2)}, u32[]{:S(2)}) collective-permute-start(bf16[128,1024]{1,0:T(8,128)(2,1)S(1)} %get-tuple-element.59), channel_id=1, source_target_pairs={{0,4},{1,5},{2,6},{3,7},{4,8},{5,9},{6,10},{7,11},{8,12},{9,13},{1... | collective-permute-start | bytes 786440 | tf_op jit(solution)/shard_map/ppermute | solution.py:29
  64.7 6.5 %collective-permute-start.13 = (bf16[128,512]{1,0:T(8,128)(2,1)S(1)}, bf16[128,512]{1,0:T(8,128)(2,1)S(1)}, u32[]{:S(2)}, u32[]{:S(2)}) collective-permute-start(bf16[128,512]{1,0:T(8,128)(2,1)S(1)} %get-tuple-element.60), channel_id=1, source_target_pairs={{0,1},{1,0},{2,3},{3,2},{4,5},{5,4},{6,7},{7,6},{8,9},{9,8},{10,11... | collective-permute-start | bytes 393224 | tf_op jit(solution)/shard_map/ppermute | solution.py:32
  65.0 7.8 %collective-permute-start.14 = (bf16[128,512]{1,0:T(8,128)(2,1)S(1)}, bf16[128,512]{1,0:T(8,128)(2,1)S(1)}, u32[]{:S(2)}, u32[]{:S(2)}) collective-permute-start(bf16[128,512]{1,0:T(8,128)(2,1)S(1)} %get-tuple-element.61), channel_id=1, source_target_pairs={{0,2},{1,3},{2,0},{3,1},{4,6},{5,7},{6,4},{7,5},{8,10},{9,11},{10,... | collective-permute-start | bytes 393224 | tf_op jit(solution)/shard_map/ppermute | solution.py:33
  68.8 8.1 %collective-permute-start.34 = (bf16[128,512]{1,0:T(8,128)(2,1)S(1)}, bf16[128,512]{1,0:T(8,128)(2,1)S(1)}, u32[]{:S(2)}, u32[]{:S(2)}) collective-permute-start(bf16[128,512]{1,0:T(8,128)(2,1)S(1)} %get-tuple-element.81), channel_id=1, source_target_pairs={{0,1},{1,0},{2,3},{3,2},{4,5},{5,4},{6,7},{7,6},{8,9},{9,8},{10,11... | collective-permute-start | bytes 393224 | tf_op jit(solution)/shard_map/ppermute | solution.py:32
  68.9 8.4 %collective-permute-start.35 = (bf16[128,512]{1,0:T(8,128)(2,1)S(1)}, bf16[128,512]{1,0:T(8,128)(2,1)S(1)}, u32[]{:S(2)}, u32[]{:S(2)}) collective-permute-start(bf16[128,512]{1,0:T(8,128)(2,1)S(1)} %get-tuple-element.82), channel_id=1, source_target_pairs={{0,2},{1,3},{2,0},{3,1},{4,6},{5,7},{6,4},{7,5},{8,10},{9,11},{10,... | collective-permute-start | bytes 393224 | tf_op jit(solution)/shard_map/ppermute | solution.py:33
  71.2 12.5 %collective-permute-start.33 = (bf16[128,1024]{1,0:T(8,128)(2,1)S(1)}, bf16[128,1024]{1,0:T(8,128)(2,1)S(1)}, u32[]{:S(2)}, u32[]{:S(2)}) collective-permute-start(bf16[128,1024]{1,0:T(8,128)(2,1)S(1)} %get-tuple-element.80), channel_id=1, source_target_pairs={{0,4},{1,5},{2,6},{3,7},{4,8},{5,9},{6,10},{7,11},{8,12},{9,13},{1... | collective-permute-start | bytes 786440 | tf_op jit(solution)/shard_map/ppermute | solution.py:29
  74.2 11.0 %collective-permute-start.15 = (bf16[128,1024]{1,0:T(8,128)(2,1)S(1)}, bf16[128,1024]{1,0:T(8,128)(2,1)S(1)}, u32[]{:S(2)}, u32[]{:S(2)}) collective-permute-start(bf16[128,1024]{1,0:T(8,128)(2,1)S(1)} %get-tuple-element.62), channel_id=1, source_target_pairs={{0,4},{1,5},{2,6},{3,7},{4,8},{5,9},{6,10},{7,11},{8,12},{9,13},{1... | collective-permute-start | bytes 786440 | tf_op jit(solution)/shard_map/ppermute | solution.py:29
  (14 other events, 90.6 us)

commit v2 on v1

--- a/solution.py
+++ b/solution.py
@@ -12,7 +12,7 @@
 STRIPS = 4
 CHUNKS = 2
 COLS = 512
-EARLY = 6
+EARLY = 4
 PARTS = 8
 SPARE = 0
 LIMIT = 16 << 20
@@ -221,25 +221,33 @@
     )(select, weights)
 
 
-def side_body(tick, chunk, near, far, seeds, patches, table, weights, out):
+def side_body(tick, chunk, start, near, seeds, patches, table, weights, out):
     loaded = amplitudes(tick, chunk, near.shape[0], seeds, patches, table)
     for low in range(0, out.shape[1], COLS):
-        out[:, low : low + COLS] = lateral(loaded, near, far, weights, table, low, low + COLS)
+        high = low + COLS
+        total = jnp.dot(
+            near[...],
+            weights[start : start + near.shape[1], low:high],
+            preferred_element_type=jnp.float32,
+        )
+        out[:, low:high] = total + lax.dot_general(
+            loaded, table[:, low:high], (((0,), (0,)), ((), ())), preferred_element_type=jnp.float32
+        )
 
 
 def side(tick, chunk, got, common, weights):
     return pl.pallas_call(
-        functools.partial(side_body, tick, chunk),
+        functools.partial(side_body, tick, chunk, got[0].shape[1]),
         out_shape=jax.ShapeDtypeStruct((got[0].shape[0], weights.shape[1]), jnp.float32),
-        in_specs=[VMEM] * 6,
+        in_specs=[VMEM] * 5,
         out_specs=VMEM,
         name="side",
         compiler_params=pltpu.CompilerParams(vmem_limit_bytes=LIMIT),
         cost_estimate=cost(got[0].shape[0] // 2, weights),
-    )(*got[1:], *common[1:], weights)
-
-
-def last_body(chunk, parts, onward, beside, *refs):
+    )(got[1], *common[1:], weights)
+
+
+def last_body(chunk, parts, onward, far, beside, weights, *refs):
     uppers = refs[:parts]
     out, buffer, sems = refs[-3:]
     rows = buffer.shape[0]
@@ -250,6 +258,9 @@
         total = beside[:, low:high] + jnp.dot(
             onward[...], upper[...], preferred_element_type=jnp.float32
         )
+        total += jnp.dot(
+            far[...], weights[weights.shape[0] - far.shape[1] :, low:high], preferred_element_type=jnp.float32
+        )
         buffer[:, low:high] = total.astype(jnp.bfloat16)
         copies.append(
             pltpu.make_async_copy(
@@ -271,17 +282,17 @@
     return pl.pallas_call(
         functools.partial(last_body, chunk, len(uppers)),
         out_shape=jax.ShapeDtypeStruct((1, rows * CHUNKS, width), jnp.bfloat16),
-        in_specs=[VMEM] * (len(uppers) + 2) + [ANY] * len(extra),
+        in_specs=[VMEM] * (len(uppers) + 4) + [ANY] * len(extra),
         out_specs=ANY,
         scratch_shapes=[
             pltpu.VMEM((rows, width), jnp.bfloat16),
             pltpu.SemaphoreType.DMA((len(uppers),)),
         ],
-        input_output_aliases={len(uppers) + 2: 0} if extra else {},
+        input_output_aliases={len(uppers) + 4: 0} if extra else {},
         name="last",
         compiler_params=pltpu.CompilerParams(vmem_limit_bytes=LIMIT),
         cost_estimate=cost(rows // 2, weights),
-    )(got[0], beside, *uppers, *extra)
+    )(got[0], got[2], beside, weights, *uppers, *extra)
 
 
 def on_device(traces, operator, loads, seeds, patches, trace_map):

time: 87 us -> 86.6 us (level)
  transfers between devices with their start and end apart: 36 -> 36, of which waited for: 10 -> 12; matrix products, arithmetic and copies ran while one was open for 0% -> 0% of each run, Pallas kernels for 33% -> 33%
where the time goes in v2:
time: 86.6 us; the launch traced here: 86.4 us
  starting transfers between devices  33.5 us (39%)
  Pallas kernels  31.6 us (36%)
  waiting for transfers between devices  20.9 us (24%)
    ppermute x12, starting transfers between devices, exchange(): lax.ppermute(onward, 'bay', [(i, (i + STRIPS) % count) for i in range(sto...  18.1 us
    ppermute x12, waiting for transfers between devices, exchange(): got_far = lax.ppermute(far, 'bay', [(i, i ^ 2) for i in range(count)])  15.5 us
    ppermute x12, starting transfers between devices, exchange(): got_far = lax.ppermute(far, 'bay', [(i, i ^ 2) for i in range(count)])  14.3 us
    pallas_call x8, Pallas kernels, step(): pl.pallas_call(functools.partial(step_body, tick, chunk), out_shape=tuple...  13.4 us
    pallas_call x8, Pallas kernels, columns_of(): pl.pallas_call(functools.partial(column_body, low), out_shape=jax.ShapeDt...  5.73 us
    ppermute x12, waiting for transfers between devices, exchange(): lax.ppermute(onward, 'bay', [(i, (i + STRIPS) % count) for i in range(sto...  5.33 us
    pallas_call x1, Pallas kernels, load(): pl.pallas_call(functools.partial(load_body, spans), out_shape=tuple(shape...  3.6 us
    pallas_call x2, Pallas kernels, last_step(): pl.pallas_call(functools.partial(last_body, chunk, len(uppers)), out_shap...  3.52 us
  transfers between devices with their start and end apart: 36, of which 12 were waited for; matrix products, arithmetic and copies ran while one was open for 0% of the time, Pallas kernels for 33%

profile of v2, /device:TPU:0, one launch (start us, length us, event | category | flops | bytes accessed | tf_op | source)
XLA Modules:
  0.0 86.4 jit_solution(17246648454745994878)
XLA Ops:
  1.2 3.1 %collective-permute-start.18 = (bf16[128,1024]{1,0:T(8,128)(2,1)S(1)}, bf16[128,1024]{1,0:T(8,128)(2,1)S(1)}, u32[]{:S(2)}, u32[]{:S(2)}) collective-permute-start(bf16[128,1024]{1,0:T(8,128)(2,1)S(1)} %get-tuple-element.65), channel_id=1, source_target_pairs={{0,4},{1,5},{2,6},{3,7},{4,8},{5,9},{6,10},{7,11},{8,12},{9,13},{1... | collective-permute-start | bytes 786440 | tf_op jit(solution)/shard_map/ppermute | solution.py:29
  7.4 3.6 %load.1 = (bf16[128,512]{1,0:T(8,128)(2,1)S(1)}, bf16[128,512]{1,0:T(8,128)(2,1)S(1)}, bf16[1024,1024]{1,0:T(8,128)(2,1)S(1)}, bf16[2048,2048]{1,0:T(8,128)(2,1)S(1)}, bf16[16,2048]{1,0:T(8,128)(2,1)S(1)}) custom-call(s32[1,1024]{1,0:T(1,128)} %trace_map.1, bf16[1,256,2048]{2,1,0:T(8,128)(2,1)} %source.3, bf16[1,2048,2048]{2,1,0:T(8,128)(2,1)} %operator.1, ...), custom_call_target="tpu_custom_call" | custom-call | tf_op jit(solution)/shard_map/load/pallas_call | solution.py:94
  11.7 1.8 %collective-permute-done.18.onward = bf16[128,1024]{1,0:T(8,128)(2,1)S(1)} collective-permute-done((bf16[128,1024]{1,0:T(8,128)(2,1)S(1)}, bf16[128,1024]{1,0:T(8,128)(2,1)S(1)}, u32[]{:S(2)}, u32[]{:S(2)}) %collective-permute-start.18) | collective-permute-done | bytes 262176 | tf_op jit(solution)/shard_map/ppermute | solution.py:29
  13.5 1.7 %shard_map.69 = (bf16[128,1024]{1,0:T(8,128)(2,1)S(1)}, bf16[128,512]{1,0:T(8,128)(2,1)S(1)}, bf16[128,512]{1,0:T(8,128)(2,1)S(1)}) custom-call(bf16[128,1024]{1,0:T(8,128)(2,1)S(1)} %collective-permute-done.18.onward, bf16[128,512]{1,0:T(8,128)(2,1)S(1)} %collective-permute-done.19.near, bf16[128,512]{1,0:T(8,128)(2,1)S(1)} %collective-permute-done.20.far, ...), custom_call_target="tpu_custom_call" | custom-call | flops 1073741824 | bytes 8388608 | tf_op jit(solution)/shard_map/pallas_call | solution.py:191
  15.4 1.7 %collective-permute-done.2.far = bf16[128,512]{1,0:T(8,128)(2,1)S(1)} collective-permute-done((bf16[128,512]{1,0:T(8,128)(2,1)S(1)}, bf16[128,512]{1,0:T(8,128)(2,1)S(1)}, u32[]{:S(2)}, u32[]{:S(2)}) %collective-permute-start.2) | collective-permute-done | bytes 131104 | tf_op jit(solution)/shard_map/ppermute | solution.py:33
  18.5 1.7 %shard_map.64 = (bf16[128,1024]{1,0:T(8,128)(2,1)S(1)}, bf16[128,512]{1,0:T(8,128)(2,1)S(1)}, bf16[128,512]{1,0:T(8,128)(2,1)S(1)}) custom-call(bf16[128,1024]{1,0:T(8,128)(2,1)S(1)} %collective-permute-done.onward, bf16[128,512]{1,0:T(8,128)(2,1)S(1)} %collective-permute-done.1.near, bf16[128,512]{1,0:T(8,128)(2,1)S(1)} %collective-permute-done.2.far, ...), custom_call_target="tpu_custom_call" | custom-call | flops 1073741824 | bytes 8388608 | tf_op jit(solution)/shard_map/pallas_call | solution.py:191
  22.4 3.4 %collective-permute-done.23.far = bf16[128,512]{1,0:T(8,128)(2,1)S(1)} collective-permute-done((bf16[128,512]{1,0:T(8,128)(2,1)S(1)}, bf16[128,512]{1,0:T(8,128)(2,1)S(1)}, u32[]{:S(2)}, u32[]{:S(2)}) %collective-permute-start.23) | collective-permute-done | bytes 131104 | tf_op jit(solution)/shard_map/ppermute | solution.py:33
  25.8 1.7 %shard_map.70 = (bf16[128,1024]{1,0:T(8,128)(2,1)S(1)}, bf16[128,512]{1,0:T(8,128)(2,1)S(1)}, bf16[128,512]{1,0:T(8,128)(2,1)S(1)}) custom-call(bf16[128,1024]{1,0:T(8,128)(2,1)S(1)} %collective-permute-done.21.onward, bf16[128,512]{1,0:T(8,128)(2,1)S(1)} %collective-permute-done.22.near, bf16[128,512]{1,0:T(8,128)(2,1)S(1)} %collective-permute-done.23.far, ...), custom_call_target="tpu_custom_call" | custom-call | flops 1073741824 | bytes 8388608 | tf_op jit(solution)/shard_map/pallas_call | solution.py:191
  27.6 2.1 %collective-permute-start.24 = (bf16[128,1024]{1,0:T(8,128)(2,1)S(1)}, bf16[128,1024]{1,0:T(8,128)(2,1)S(1)}, u32[]{:S(2)}, u32[]{:S(2)}) collective-permute-start(bf16[128,1024]{1,0:T(8,128)(2,1)S(1)} %get-tuple-element.71), channel_id=1, source_target_pairs={{0,4},{1,5},{2,6},{3,7},{4,8},{5,9},{6,10},{7,11},{8,12},{9,13},{1... | collective-permute-start | bytes 786440 | tf_op jit(solution)/shard_map/ppermute | solution.py:29
  29.6 1.7 %shard_map.65 = (bf16[128,1024]{1,0:T(8,128)(2,1)S(1)}, bf16[128,512]{1,0:T(8,128)(2,1)S(1)}, bf16[128,512]{1,0:T(8,128)(2,1)S(1)}) custom-call(bf16[128,1024]{1,0:T(8,128)(2,1)S(1)} %collective-permute-done.3.onward, bf16[128,512]{1,0:T(8,128)(2,1)S(1)} %collective-permute-done.4.near, bf16[128,512]{1,0:T(8,128)(2,1)S(1)} %collective-permute-done.5.far, ...), custom_call_target="tpu_custom_call" | custom-call | flops 1073741824 | bytes 8388608 | tf_op jit(solution)/shard_map/pallas_call | solution.py:191
  31.3 1.6 %collective-permute-start.6 = (bf16[128,1024]{1,0:T(8,128)(2,1)S(1)}, bf16[128,1024]{1,0:T(8,128)(2,1)S(1)}, u32[]{:S(2)}, u32[]{:S(2)}) collective-permute-start(bf16[128,1024]{1,0:T(8,128)(2,1)S(1)} %get-tuple-element.53), channel_id=1, source_target_pairs={{0,4},{1,5},{2,6},{3,7},{4,8},{5,9},{6,10},{7,11},{8,12},{9,13},{1... | collective-permute-start | bytes 786440 | tf_op jit(solution)/shard_map/ppermute | solution.py:29
  33.0 2.5 %collective-permute-start.26 = (bf16[128,512]{1,0:T(8,128)(2,1)S(1)}, bf16[128,512]{1,0:T(8,128)(2,1)S(1)}, u32[]{:S(2)}, u32[]{:S(2)}) collective-permute-start(bf16[128,512]{1,0:T(8,128)(2,1)S(1)} %get-tuple-element.73), channel_id=1, source_target_pairs={{0,2},{1,3},{2,0},{3,1},{4,6},{5,7},{6,4},{7,5},{8,10},{9,11},{10,... | collective-permute-start | bytes 393224 | tf_op jit(solution)/shard_map/ppermute | solution.py:33
  35.5 3.9 %collective-permute-done.26.far = bf16[128,512]{1,0:T(8,128)(2,1)S(1)} collective-permute-done((bf16[128,512]{1,0:T(8,128)(2,1)S(1)}, bf16[128,512]{1,0:T(8,128)(2,1)S(1)}, u32[]{:S(2)}, u32[]{:S(2)}) %collective-permute-start.26) | collective-permute-done | bytes 131104 | tf_op jit(solution)/shard_map/ppermute | solution.py:33
  39.4 1.7 %shard_map.71 = (bf16[128,1024]{1,0:T(8,128)(2,1)S(1)}, bf16[128,512]{1,0:T(8,128)(2,1)S(1)}, bf16[128,512]{1,0:T(8,128)(2,1)S(1)}) custom-call(bf16[128,1024]{1,0:T(8,128)(2,1)S(1)} %collective-permute-done.24.onward, bf16[128,512]{1,0:T(8,128)(2,1)S(1)} %collective-permute-done.25.near, bf16[128,512]{1,0:T(8,128)(2,1)S(1)} %collective-permute-done.26.far, ...), custom_call_target="tpu_custom_call" | custom-call | flops 1073741824 | bytes 8388608 | tf_op jit(solution)/shard_map/pallas_call | solution.py:191
  43.9 1.7 %shard_map.66 = (bf16[128,1024]{1,0:T(8,128)(2,1)S(1)}, bf16[128,512]{1,0:T(8,128)(2,1)S(1)}, bf16[128,512]{1,0:T(8,128)(2,1)S(1)}) custom-call(bf16[128,1024]{1,0:T(8,128)(2,1)S(1)} %collective-permute-done.6.onward, bf16[128,512]{1,0:T(8,128)(2,1)S(1)} %collective-permute-done.7.near, bf16[128,512]{1,0:T(8,128)(2,1)S(1)} %collective-permute-done.8.far, ...), custom_call_target="tpu_custom_call" | custom-call | flops 1073741824 | bytes 8388608 | tf_op jit(solution)/shard_map/pallas_call | solution.py:191
  46.6 3.0 %collective-permute-start.29 = (bf16[128,512]{1,0:T(8,128)(2,1)S(1)}, bf16[128,512]{1,0:T(8,128)(2,1)S(1)}, u32[]{:S(2)}, u32[]{:S(2)}) collective-permute-start(bf16[128,512]{1,0:T(8,128)(2,1)S(1)} %get-tuple-element.76), channel_id=1, source_target_pairs={{0,2},{1,3},{2,0},{3,1},{4,6},{5,7},{6,4},{7,5},{8,10},{9,11},{10,... | collective-permute-start | bytes 393224 | tf_op jit(solution)/shard_map/ppermute | solution.py:33
  53.8 1.7 %shard_map.72 = (bf16[128,1024]{1,0:T(8,128)(2,1)S(1)}, bf16[128,512]{1,0:T(8,128)(2,1)S(1)}, bf16[128,512]{1,0:T(8,128)(2,1)S(1)}) custom-call(bf16[128,1024]{1,0:T(8,128)(2,1)S(1)} %collective-permute-done.27.onward, bf16[128,512]{1,0:T(8,128)(2,1)S(1)} %collective-permute-done.28.near, bf16[128,512]{1,0:T(8,128)(2,1)S(1)} %collective-permute-done.29.far, ...), custom_call_target="tpu_custom_call" | custom-call | flops 1073741824 | bytes 8388608 | tf_op jit(solution)/shard_map/pallas_call | solution.py:191
  55.5 1.6 %collective-permute-start.30 = (bf16[128,1024]{1,0:T(8,128)(2,1)S(1)}, bf16[128,1024]{1,0:T(8,128)(2,1)S(1)}, u32[]{:S(2)}, u32[]{:S(2)}) collective-permute-start(bf16[128,1024]{1,0:T(8,128)(2,1)S(1)} %get-tuple-element.77), channel_id=1, source_target_pairs={{0,4},{1,5},{2,6},{3,7},{4,8},{5,9},{6,10},{7,11},{8,12},{9,13},{1... | collective-permute-start | bytes 786440 | tf_op jit(solution)/shard_map/ppermute | solution.py:29
  57.1 1.7 %shard_map.67 = (bf16[128,1024]{1,0:T(8,128)(2,1)S(1)}, bf16[128,512]{1,0:T(8,128)(2,1)S(1)}, bf16[128,512]{1,0:T(8,128)(2,1)S(1)}) custom-call(bf16[128,1024]{1,0:T(8,128)(2,1)S(1)} %collective-permute-done.9.onward, bf16[128,512]{1,0:T(8,128)(2,1)S(1)} %collective-permute-done.10.near, bf16[128,512]{1,0:T(8,128)(2,1)S(1)} %collective-permute-done.11.far, ...), custom_call_target="tpu_custom_call" | custom-call | flops 1073741824 | bytes 8388608 | tf_op jit(solution)/shard_map/pallas_call | solution.py:191
  61.1 2.0 %collective-permute-start.32 = (bf16[128,512]{1,0:T(8,128)(2,1)S(1)}, bf16[128,512]{1,0:T(8,128)(2,1)S(1)}, u32[]{:S(2)}, u32[]{:S(2)}) collective-permute-start(bf16[128,512]{1,0:T(8,128)(2,1)S(1)} %get-tuple-element.79), channel_id=1, source_target_pairs={{0,2},{1,3},{2,0},{3,1},{4,6},{5,7},{6,4},{7,5},{8,10},{9,11},{10,... | collective-permute-start | bytes 393224 | tf_op jit(solution)/shard_map/ppermute | solution.py:33
  72.5 3.1 %collective-permute-start.15 = (bf16[128,1024]{1,0:T(8,128)(2,1)S(1)}, bf16[128,1024]{1,0:T(8,128)(2,1)S(1)}, u32[]{:S(2)}, u32[]{:S(2)}) collective-permute-start(bf16[128,1024]{1,0:T(8,128)(2,1)S(1)} %get-tuple-element.62), channel_id=1, source_target_pairs={{0,4},{1,5},{2,6},{3,7},{4,8},{5,9},{6,10},{7,11},{8,12},{9,13},{1... | collective-permute-start | bytes 786440 | tf_op jit(solution)/shard_map/ppermute | solution.py:29
  79.1 3.1 %collective-permute-done.34.far = bf16[128,512]{1,0:T(8,128)(2,1)S(1)} collective-permute-done((bf16[128,512]{1,0:T(8,128)(2,1)S(1)}, bf16[128,512]{1,0:T(8,128)(2,1)S(1)}, u32[]{:S(2)}, u32[]{:S(2)}) %collective-permute-start.34) | collective-permute-done | bytes 131104 | tf_op jit(solution)/shard_map/ppermute | solution.py:33
  82.2 1.8 %last.2.refs_8_ = bf16[1,256,2048]{2,1,0:T(8,128)(2,1)} custom-call(bf16[128,1024]{1,0:T(8,128)(2,1)S(1)} %collective-permute-done.33.onward, bf16[128,512]{1,0:T(8,128)(2,1)S(1)} %collective-permute-done.34.far, f32[128,2048]{1,0:T(8,128)S(1)} %side.3.beside, bf16[2048,2048]{1,0:T(8,128)(2,1)S(1)} %get-tuple-element.49.weights, ...), custom_call_target="tpu_custom_call" | custom-call | flops 536870912 | bytes 8388608 | tf_op jit(solution)/shard_map/last/pallas_call | solution.py:282
  84.4 1.8 %last.3 = bf16[1,256,2048]{2,1,0:T(8,128)(2,1)} custom-call(bf16[128,1024]{1,0:T(8,128)(2,1)S(1)} %collective-permute-done.15.onward, bf16[128,512]{1,0:T(8,128)(2,1)S(1)} %collective-permute-done.16.far, f32[128,2048]{1,0:T(8,128)S(1)} %side.2.beside, bf16[2048,2048]{1,0:T(8,128)(2,1)S(1)} %get-tuple-element.49.weights, ...), custom_call_target="tpu_custom_call", output_to_operand_aliasing={{}: (12, {})} | custom-call | flops 536870912 | bytes 8388608 | tf_op jit(solution)/shard_map/last/pallas_call | solution.py:282
  (76 shorter events, 32.4 us)
Async XLA Ops:
  1.2 12.3 %collective-permute-start.18 = (bf16[128,1024]{1,0:T(8,128)(2,1)S(1)}, bf16[128,1024]{1,0:T(8,128)(2,1)S(1)}, u32[]{:S(2)}, u32[]{:S(2)}) collective-permute-start(bf16[128,1024]{1,0:T(8,128)(2,1)S(1)} %get-tuple-element.65), channel_id=1, source_target_pairs={{0,4},{1,5},{2,6},{3,7},{4,8},{5,9},{6,10},{7,11},{8,12},{9,13},{1... | collective-permute-start | bytes 786440 | tf_op jit(solution)/shard_map/ppermute | solution.py:29
  4.3 6.8 %collective-permute-start.19 = (bf16[128,512]{1,0:T(8,128)(2,1)S(1)}, bf16[128,512]{1,0:T(8,128)(2,1)S(1)}, u32[]{:S(2)}, u32[]{:S(2)}) collective-permute-start(bf16[128,512]{1,0:T(8,128)(2,1)S(1)} %get-tuple-element.66), channel_id=1, source_target_pairs={{0,1},{1,0},{2,3},{3,2},{4,5},{5,4},{6,7},{7,6},{8,9},{9,8},{10,11... | collective-permute-start | bytes 393224 | tf_op jit(solution)/shard_map/ppermute | solution.py:32
  4.3 14.1 %collective-permute-start = (bf16[128,1024]{1,0:T(8,128)(2,1)S(1)}, bf16[128,1024]{1,0:T(8,128)(2,1)S(1)}, u32[]{:S(2)}, u32[]{:S(2)}) collective-permute-start(bf16[128,1024]{1,0:T(8,128)(2,1)S(1)} %get-tuple-element.44), channel_id=1, source_target_pairs={{0,4},{1,5},{2,6},{3,7},{4,8},{5,9},{6,10},{7,11},{8,12},{9,13},{1... | collective-permute-start | bytes 786440 | tf_op jit(solution)/shard_map/ppermute | solution.py:29
  15.2 10.6 %collective-permute-start.21 = (bf16[128,1024]{1,0:T(8,128)(2,1)S(1)}, bf16[128,1024]{1,0:T(8,128)(2,1)S(1)}, u32[]{:S(2)}, u32[]{:S(2)}) collective-permute-start(bf16[128,1024]{1,0:T(8,128)(2,1)S(1)} %get-tuple-element.68), channel_id=1, source_target_pairs={{0,4},{1,5},{2,6},{3,7},{4,8},{5,9},{6,10},{7,11},{8,12},{9,13},{1... | collective-permute-start | bytes 786440 | tf_op jit(solution)/shard_map/ppermute | solution.py:29
  15.3 6.6 %collective-permute-start.22 = (bf16[128,512]{1,0:T(8,128)(2,1)S(1)}, bf16[128,512]{1,0:T(8,128)(2,1)S(1)}, u32[]{:S(2)}, u32[]{:S(2)}) collective-permute-start(bf16[128,512]{1,0:T(8,128)(2,1)S(1)} %get-tuple-element.69), channel_id=1, source_target_pairs={{0,1},{1,0},{2,3},{3,2},{4,5},{5,4},{6,7},{7,6},{8,9},{9,8},{10,11... | collective-permute-start | bytes 393224 | tf_op jit(solution)/shard_map/ppermute | solution.py:32
  20.2 9.5 %collective-permute-start.3 = (bf16[128,1024]{1,0:T(8,128)(2,1)S(1)}, bf16[128,1024]{1,0:T(8,128)(2,1)S(1)}, u32[]{:S(2)}, u32[]{:S(2)}) collective-permute-start(bf16[128,1024]{1,0:T(8,128)(2,1)S(1)} %get-tuple-element.50), channel_id=1, source_target_pairs={{0,4},{1,5},{2,6},{3,7},{4,8},{5,9},{6,10},{7,11},{8,12},{9,13},{1... | collective-permute-start | bytes 786440 | tf_op jit(solution)/shard_map/ppermute | solution.py:29
  21.9 7.7 %collective-permute-start.4 = (bf16[128,512]{1,0:T(8,128)(2,1)S(1)}, bf16[128,512]{1,0:T(8,128)(2,1)S(1)}, u32[]{:S(2)}, u32[]{:S(2)}) collective-permute-start(bf16[128,512]{1,0:T(8,128)(2,1)S(1)} %get-tuple-element.51), channel_id=1, source_target_pairs={{0,1},{1,0},{2,3},{3,2},{4,5},{5,4},{6,7},{7,6},{8,9},{9,8},{10,11... | collective-permute-start | bytes 393224 | tf_op jit(solution)/shard_map/ppermute | solution.py:32
  21.9 7.7 %collective-permute-start.5 = (bf16[128,512]{1,0:T(8,128)(2,1)S(1)}, bf16[128,512]{1,0:T(8,128)(2,1)S(1)}, u32[]{:S(2)}, u32[]{:S(2)}) collective-permute-start(bf16[128,512]{1,0:T(8,128)(2,1)S(1)} %get-tuple-element.52), channel_id=1, source_target_pairs={{0,2},{1,3},{2,0},{3,1},{4,6},{5,7},{6,4},{7,5},{8,10},{9,11},{10,... | collective-permute-start | bytes 393224 | tf_op jit(solution)/shard_map/ppermute | solution.py:33
  27.5 8.0 %collective-permute-start.25 = (bf16[128,512]{1,0:T(8,128)(2,1)S(1)}, bf16[128,512]{1,0:T(8,128)(2,1)S(1)}, u32[]{:S(2)}, u32[]{:S(2)}) collective-permute-start(bf16[128,512]{1,0:T(8,128)(2,1)S(1)} %get-tuple-element.72), channel_id=1, source_target_pairs={{0,1},{1,0},{2,3},{3,2},{4,5},{5,4},{6,7},{7,6},{8,9},{9,8},{10,11... | collective-permute-start | bytes 393224 | tf_op jit(solution)/shard_map/ppermute | solution.py:32
  27.6 11.9 %collective-permute-start.24 = (bf16[128,1024]{1,0:T(8,128)(2,1)S(1)}, bf16[128,1024]{1,0:T(8,128)(2,1)S(1)}, u32[]{:S(2)}, u32[]{:S(2)}) collective-permute-start(bf16[128,1024]{1,0:T(8,128)(2,1)S(1)} %get-tuple-element.71), channel_id=1, source_target_pairs={{0,4},{1,5},{2,6},{3,7},{4,8},{5,9},{6,10},{7,11},{8,12},{9,13},{1... | collective-permute-start | bytes 786440 | tf_op jit(solution)/shard_map/ppermute | solution.py:29
  31.3 12.6 %collective-permute-start.6 = (bf16[128,1024]{1,0:T(8,128)(2,1)S(1)}, bf16[128,1024]{1,0:T(8,128)(2,1)S(1)}, u32[]{:S(2)}, u32[]{:S(2)}) collective-permute-start(bf16[128,1024]{1,0:T(8,128)(2,1)S(1)} %get-tuple-element.53), channel_id=1, source_target_pairs={{0,4},{1,5},{2,6},{3,7},{4,8},{5,9},{6,10},{7,11},{8,12},{9,13},{1... | collective-permute-start | bytes 786440 | tf_op jit(solution)/shard_map/ppermute | solution.py:29
  33.0 6.4 %collective-permute-start.26 = (bf16[128,512]{1,0:T(8,128)(2,1)S(1)}, bf16[128,512]{1,0:T(8,128)(2,1)S(1)}, u32[]{:S(2)}, u32[]{:S(2)}) collective-permute-start(bf16[128,512]{1,0:T(8,128)(2,1)S(1)} %get-tuple-element.73), channel_id=1, source_target_pairs={{0,2},{1,3},{2,0},{3,1},{4,6},{5,7},{6,4},{7,5},{8,10},{9,11},{10,... | collective-permute-start | bytes 393224 | tf_op jit(solution)/shard_map/ppermute | solution.py:33
  35.4 7.0 %collective-permute-start.7 = (bf16[128,512]{1,0:T(8,128)(2,1)S(1)}, bf16[128,512]{1,0:T(8,128)(2,1)S(1)}, u32[]{:S(2)}, u32[]{:S(2)}) collective-permute-start(bf16[128,512]{1,0:T(8,128)(2,1)S(1)} %get-tuple-element.54), channel_id=1, source_target_pairs={{0,1},{1,0},{2,3},{3,2},{4,5},{5,4},{6,7},{7,6},{8,9},{9,8},{10,11... | collective-permute-start | bytes 393224 | tf_op jit(solution)/shard_map/ppermute | solution.py:32
  35.4 7.0 %collective-permute-start.8 = (bf16[128,512]{1,0:T(8,128)(2,1)S(1)}, bf16[128,512]{1,0:T(8,128)(2,1)S(1)}, u32[]{:S(2)}, u32[]{:S(2)}) collective-permute-start(bf16[128,512]{1,0:T(8,128)(2,1)S(1)} %get-tuple-element.55), channel_id=1, source_target_pairs={{0,2},{1,3},{2,0},{3,1},{4,6},{5,7},{6,4},{7,5},{8,10},{9,11},{10,... | collective-permute-start | bytes 393224 | tf_op jit(solution)/shard_map/ppermute | solution.py:33
  41.1 12.7 %collective-permute-start.27 = (bf16[128,1024]{1,0:T(8,128)(2,1)S(1)}, bf16[128,1024]{1,0:T(8,128)(2,1)S(1)}, u32[]{:S(2)}, u32[]{:S(2)}) collective-permute-start(bf16[128,1024]{1,0:T(8,128)(2,1)S(1)} %get-tuple-element.74), channel_id=1, source_target_pairs={{0,4},{1,5},{2,6},{3,7},{4,8},{5,9},{6,10},{7,11},{8,12},{9,13},{1... | collective-permute-start | bytes 786440 | tf_op jit(solution)/shard_map/ppermute | solution.py:29
  45.6 11.5 %collective-permute-start.9 = (bf16[128,1024]{1,0:T(8,128)(2,1)S(1)}, bf16[128,1024]{1,0:T(8,128)(2,1)S(1)}, u32[]{:S(2)}, u32[]{:S(2)}) collective-permute-start(bf16[128,1024]{1,0:T(8,128)(2,1)S(1)} %get-tuple-element.56), channel_id=1, source_target_pairs={{0,4},{1,5},{2,6},{3,7},{4,8},{5,9},{6,10},{7,11},{8,12},{9,13},{1... | collective-permute-start | bytes 786440 | tf_op jit(solution)/shard_map/ppermute | solution.py:29
  46.6 7.1 %collective-permute-start.29 = (bf16[128,512]{1,0:T(8,128)(2,1)S(1)}, bf16[128,512]{1,0:T(8,128)(2,1)S(1)}, u32[]{:S(2)}, u32[]{:S(2)}) collective-permute-start(bf16[128,512]{1,0:T(8,128)(2,1)S(1)} %get-tuple-element.76), channel_id=1, source_target_pairs={{0,2},{1,3},{2,0},{3,1},{4,6},{5,7},{6,4},{7,5},{8,10},{9,11},{10,... | collective-permute-start | bytes 393224 | tf_op jit(solution)/shard_map/ppermute | solution.py:33
  55.5 11.8 %collective-permute-start.30 = (bf16[128,1024]{1,0:T(8,128)(2,1)S(1)}, bf16[128,1024]{1,0:T(8,128)(2,1)S(1)}, u32[]{:S(2)}, u32[]{:S(2)}) collective-permute-start(bf16[128,1024]{1,0:T(8,128)(2,1)S(1)} %get-tuple-element.77), channel_id=1, source_target_pairs={{0,4},{1,5},{2,6},{3,7},{4,8},{5,9},{6,10},{7,11},{8,12},{9,13},{1... | collective-permute-start | bytes 786440 | tf_op jit(solution)/shard_map/ppermute | solution.py:29
  58.8 12.3 %collective-permute-start.12 = (bf16[128,1024]{1,0:T(8,128)(2,1)S(1)}, bf16[128,1024]{1,0:T(8,128)(2,1)S(1)}, u32[]{:S(2)}, u32[]{:S(2)}) collective-permute-start(bf16[128,1024]{1,0:T(8,128)(2,1)S(1)} %get-tuple-element.59), channel_id=1, source_target_pairs={{0,4},{1,5},{2,6},{3,7},{4,8},{5,9},{6,10},{7,11},{8,12},{9,13},{1... | collective-permute-start | bytes 786440 | tf_op jit(solution)/shard_map/ppermute | solution.py:29
  68.7 8.4 %collective-permute-start.35 = (bf16[128,512]{1,0:T(8,128)(2,1)S(1)}, bf16[128,512]{1,0:T(8,128)(2,1)S(1)}, u32[]{:S(2)}, u32[]{:S(2)}) collective-permute-start(bf16[128,512]{1,0:T(8,128)(2,1)S(1)} %get-tuple-element.82), channel_id=1, source_target_pairs={{0,1},{1,0},{2,3},{3,2},{4,5},{5,4},{6,7},{7,6},{8,9},{9,8},{10,11... | collective-permute-start | bytes 393224 | tf_op jit(solution)/shard_map/ppermute | solution.py:32
  68.8 13.4 %collective-permute-start.33 = (bf16[128,1024]{1,0:T(8,128)(2,1)S(1)}, bf16[128,1024]{1,0:T(8,128)(2,1)S(1)}, u32[]{:S(2)}, u32[]{:S(2)}) collective-permute-start(bf16[128,1024]{1,0:T(8,128)(2,1)S(1)} %get-tuple-element.80), channel_id=1, source_target_pairs={{0,4},{1,5},{2,6},{3,7},{4,8},{5,9},{6,10},{7,11},{8,12},{9,13},{1... | collective-permute-start | bytes 786440 | tf_op jit(solution)/shard_map/ppermute | solution.py:29
  72.5 11.9 %collective-permute-start.15 = (bf16[128,1024]{1,0:T(8,128)(2,1)S(1)}, bf16[128,1024]{1,0:T(8,128)(2,1)S(1)}, u32[]{:S(2)}, u32[]{:S(2)}) collective-permute-start(bf16[128,1024]{1,0:T(8,128)(2,1)S(1)} %get-tuple-element.62), channel_id=1, source_target_pairs={{0,4},{1,5},{2,6},{3,7},{4,8},{5,9},{6,10},{7,11},{8,12},{9,13},{1... | collective-permute-start | bytes 786440 | tf_op jit(solution)/shard_map/ppermute | solution.py:29
  75.7 6.4 %collective-permute-start.34 = (bf16[128,512]{1,0:T(8,128)(2,1)S(1)}, bf16[128,512]{1,0:T(8,128)(2,1)S(1)}, u32[]{:S(2)}, u32[]{:S(2)}) collective-permute-start(bf16[128,512]{1,0:T(8,128)(2,1)S(1)} %get-tuple-element.81), channel_id=1, source_target_pairs={{0,2},{1,3},{2,0},{3,1},{4,6},{5,7},{6,4},{7,5},{8,10},{9,11},{10,... | collective-permute-start | bytes 393224 | tf_op jit(solution)/shard_map/ppermute | solution.py:33
  77.1 7.3 %collective-permute-start.16 = (bf16[128,512]{1,0:T(8,128)(2,1)S(1)}, bf16[128,512]{1,0:T(8,128)(2,1)S(1)}, u32[]{:S(2)}, u32[]{:S(2)}) collective-permute-start(bf16[128,512]{1,0:T(8,128)(2,1)S(1)} %get-tuple-element.63), channel_id=1, source_target_pairs={{0,2},{1,3},{2,0},{3,1},{4,6},{5,7},{6,4},{7,5},{8,10},{9,11},{10,... | collective-permute-start | bytes 393224 | tf_op jit(solution)/shard_map/ppermute | solution.py:33
  (14 other events, 90.8 us)
